TPU v7x, 32 devices: a whole 2x2x4 slice. The times are simulated.
32 devices in a mesh: mat: 4 (over x, core), frac: 8 (over z, y).
Axes of the slice: x: 2, y: 2, z: 4, core: 2. Of those that a mesh axis runs over, the one named last changes fastest.
Arguments:
- pressure_start: float32 [64, 512, 256], P('mat', 'frac'), may hold values from -6 to 6
- face_trans: float32 [3, 64, 512, 256], P(None, 'mat', 'frac'), may hold values from 0.2 to 2
- cell_coef: float32 [64, 512, 256], P('mat', 'frac'), may hold values from 0.05 to 0.5
- matrix_source: float32 [64, 512, 256], P('mat', 'frac'), may hold values from -6 to 6
- mortar_owner: int32 [16384, 1], P(('mat', 'frac')), may hold values from 0 to 31; in each aligned block of 512 rows (0 to 511, 512 to 1023, ...) at most 32 rows name the same one
- mortar_cell: int32 [16384], P(('mat', 'frac')), may hold values from 0 to 262143
- mortar_frac: int32 [16384], P(('mat', 'frac')), may hold values from 0 to 8191
- mortar_kappa: float32 [16384], P(('mat', 'frac')), may hold values from 0.5 to 2
- tiles: float32 [64, 4, 128, 128], P('frac'), may hold values from -0.25 to 0.25
- tile_cols: int32 [64, 4], P('frac'), may hold values from 0 to 63
- frac_diag: float32 [8192], P('frac'), may hold values from 4 to 8
- frac_source: float32 [8192], P('frac'), may hold values from -6 to 6
- fracture_start: float32 [8192], P('frac'), may hold values from -6 to 6
Outputs:
- pressure: float32 [64, 512, 256], P('mat', 'frac')
- fracture: float32 [8192], P('frac')
- flux: float32 [16384], P(('mat', 'frac'))
Inputs may be any that keep to these rules, and one draw needn't show every extreme that they name: `mortar_owner`: among the 512 mortar cells of one device, at most 32 name the same owner, and in some devices some owner is named exactly 32 times.
All inputs are finite; a program needn't handle non-finite values.
Results may differ from a plain program's by a relative error of at most 0.00015.
Values sent between devices are 32-bit elements; how exact they have to be, the bound alone decides.
A program may use at most 128 MiB of HBM per device.

v0:
```python
import jax
import jax.numpy as jnp
from jax import lax
from jax.sharding import PartitionSpec as P

SWEEPS = 2
CG_ITERS = 3
OUTER = 2


relax_weight = 0.8


def shifted(value, axis, steps):
    count = lax.axis_size(axis)
    leading, last = (max(0, -steps), min(count, count - steps))
    return lax.ppermute(value, axis, [(source, source + steps) for source in range(leading, last)])


def with_halo(block, sides, width):
    for axis, dim in sides:
        count = lax.axis_size(axis)
        forward = [(i, i + 1) for i in range(count - 1)]
        backward = [(target, source) for source, target in forward]
        low = lax.ppermute(
            lax.slice_in_dim(block, block.shape[dim] - width, None, axis=dim), axis, forward
        )
        high = lax.ppermute(lax.slice_in_dim(block, 0, width, axis=dim), axis, backward)
        block = jnp.concatenate([low, block, high], axis=dim)
    return block


def shift_next(values, along):
    padding = [(0, 0)] * values.ndim
    padding[along] = (0, 1)
    return lax.slice_in_dim(jnp.pad(values, padding), 1, values.shape[along] + 1, axis=along)


def shift_prev(values, along):
    padding = [(0, 0)] * values.ndim
    padding[along] = (1, 0)
    return lax.slice_in_dim(jnp.pad(values, padding), 0, values.shape[along], axis=along)


def relax(padded, coef_part, source_part, inside):
    centre = padded[1:-1, 1:-1]
    tx_here = coef_part[0, 1:-1, 1:-1]
    tx_low = coef_part[0, :-2, 1:-1]
    ty_here = coef_part[1, 1:-1, 1:-1]
    ty_low = coef_part[1, 1:-1, :-2]
    tz_here = coef_part[2, 1:-1, 1:-1]
    tz_low = shift_prev(tz_here, 2)
    cell_part = coef_part[3, 1:-1, 1:-1]
    base_part = coef_part[4, 1:-1, 1:-1]
    diagonal = cell_part + tx_here + tx_low + ty_here + ty_low + tz_here + tz_low
    diagonal = jnp.where(inside, diagonal, 1.0)
    applied = (
        diagonal * centre
        - tx_here * padded[2:, 1:-1]
        - tx_low * padded[:-2, 1:-1]
        - ty_here * padded[1:-1, 2:]
        - ty_low * padded[1:-1, :-2]
        - tz_here * shift_next(centre, 2)
        - tz_low * shift_prev(centre, 2)
    )
    updated = centre + relax_weight * (base_part + source_part - applied) / diagonal
    return jnp.where(inside, updated, 0.0)


def body(
    pressure_start,
    face_trans,
    cell_coef,
    matrix_source,
    mortar_owner,
    mortar_cell,
    mortar_frac,
    mortar_kappa,
    tiles,
    tile_cols,
    frac_diag,
    frac_source,
    fracture_start,
):
    width_x, width_y, depth_z = pressure_start.shape
    cells = width_x * width_y * depth_z
    mat_count = lax.axis_size("mat")
    frac_count = lax.axis_size("frac")
    devices = mat_count * frac_count
    row_mat = lax.axis_index("mat")
    row_frac = lax.axis_index("frac")
    size_b = tiles.shape[2]
    coefs = jnp.concatenate([face_trans, cell_coef[None], matrix_source[None]], 0)
    lower_x = shifted(face_trans[0, -1], "mat", 1)
    lower_y = shifted(face_trans[1, :, -1], "frac", 1)
    coef_ext = jnp.pad(coefs, ((0, 0), (1, 1), (1, 1), (0, 0)))
    coef_ext = coef_ext.at[0, 0, 1:-1].set(lower_x)
    coef_ext = coef_ext.at[1, 1:-1, 0].set(lower_y)
    owner = mortar_owner[:, 0]
    mortar_count = owner.shape[0]
    capacity = max(2, 2 * mortar_count // devices)
    hits = (owner[:, None] == jnp.arange(devices, dtype=jnp.int32)[None, :]).astype(jnp.int32)
    ranks = jnp.cumsum(hits, axis=0)
    slot = jnp.sum(ranks * hits, axis=1) - 1
    place = owner * capacity + slot
    index_slots = (
        jnp.full((devices * capacity,), cells, jnp.int32)
        .at[place]
        .set(mortar_cell)
        .reshape(devices, capacity)
    )
    asked = lax.all_to_all(index_slots, ("mat", "frac"), split_axis=0, concat_axis=0, tiled=True)
    asked_safe = jnp.minimum(asked, cells - 1)

    def fracture_apply(vector):
        whole = lax.all_gather(vector, "frac", axis=0, tiled=True)
        blocks = whole.reshape(-1, size_b)
        forward = jnp.einsum(
            "rtij,rtj->ri", tiles, blocks[tile_cols], precision=lax.Precision.HIGHEST
        )
        backward = jnp.einsum(
            "rtij,ri->rtj", tiles, vector.reshape(-1, size_b), precision=lax.Precision.HIGHEST
        )
        spread = jnp.zeros_like(blocks).at[tile_cols.reshape(-1)].add(backward.reshape(-1, size_b))
        returned = lax.psum_scatter(spread, "frac", scatter_dimension=0, tiled=True)
        return frac_diag * vector + 0.5 * (forward + returned).reshape(-1)

    def two_products(residual, image):
        return lax.psum((jnp.sum(residual * residual), jnp.sum(residual * image)), "frac")

    def solve_fracture(fracture, target):
        residual = target - fracture_apply(fracture)
        image = fracture_apply(residual)
        norm_now, product = two_products(residual, image)
        alpha = norm_now / product
        direction, along_image = (residual, image)
        for step in range(CG_ITERS):
            fracture = fracture + alpha * direction
            residual = residual - alpha * along_image
            if step + 1 < CG_ITERS:
                image = fracture_apply(residual)
                norm_next, product = two_products(residual, image)
                ratio = norm_next / norm_now
                alpha = norm_next / (product - ratio * norm_next / alpha)
                direction = residual + ratio * direction
                along_image = image + ratio * along_image
                norm_now = norm_next
        return fracture

    pressure = pressure_start
    fracture = fracture_start
    flux = jnp.zeros(mortar_kappa.shape, jnp.float32)
    for outer_no in range(OUTER):
        local_values = pressure.reshape(-1)[asked_safe]
        returned = lax.all_to_all(
            local_values, ("mat", "frac"), split_axis=0, concat_axis=0, tiled=True
        )
        trace = returned.reshape(-1)[place]
        fracture_whole = lax.all_gather(fracture, "frac", axis=0, tiled=True)
        flux = mortar_kappa * (trace - fracture_whole[mortar_frac])
        landed = jax.ops.segment_sum(flux, mortar_frac, num_segments=fracture_whole.shape[0])
        summed = lax.psum(landed, ("mat", "frac"))
        load = lax.dynamic_slice_in_dim(summed, row_frac * fracture.shape[0], fracture.shape[0])
        fracture = solve_fracture(fracture, frac_source + load)
        flux_slots = (
            jnp.zeros((devices * capacity,), jnp.float32)
            .at[place]
            .set(flux)
            .reshape(devices, capacity)
        )
        arrived = lax.all_to_all(
            flux_slots, ("mat", "frac"), split_axis=0, concat_axis=0, tiled=True
        )
        source = jax.ops.segment_sum(
            arrived.reshape(-1), asked_safe.reshape(-1), num_segments=cells
        ).reshape(pressure.shape)
        for sweep_no in range(SWEEPS):
            padded = with_halo(pressure, (("mat", 0), ("frac", 1)), 1)
            global_x = row_mat * width_x - 0 + jnp.arange(width_x)
            global_y = row_frac * width_y - 0 + jnp.arange(width_y)
            keep_x = (global_x >= 0) & (global_x < width_x * mat_count)
            keep_y = (global_y >= 0) & (global_y < width_y * frac_count)
            pressure = relax(
                padded, coef_ext, source, (keep_x[:, None] & keep_y[None, :])[:, :, None]
            )
    return (pressure, fracture, flux)


def solution(mesh):
    in_specs = (
        P("mat", "frac", None),
        P(None, "mat", "frac", None),
        P("mat", "frac", None),
        P("mat", "frac", None),
        P(("mat", "frac"), None),
        P(("mat", "frac")),
        P(("mat", "frac")),
        P(("mat", "frac")),
        P("frac", None, None, None),
        P("frac", None),
        P("frac"),
        P("frac"),
        P("frac"),
    )
    out_specs = (P("mat", "frac", None), P("frac"), P(("mat", "frac")))
    return jax.shard_map(body, mesh=mesh, in_specs=in_specs, out_specs=out_specs, check_vma=False)
```

profile of v0, /device:TPU:0, one launch (start us, length us, event | category | flops | bytes accessed | tf_op | source)
XLA Modules:
  0.0 979.0 jit_solution(13991142482101642097)
XLA Ops:
  30.5 31.1 %all_gather.26 = f32[8192]{0:T(1024)S(1)} all-gather(f32[1024]{0:T(1024)} %param.29), channel_id=1, replica_groups=mesh['mat'=4,'frac'=8] {'frac'}, dimensions={0}, use_global_device_ids=true | all-gather | bytes 36864 | tf_op jit(solution)/shard_map/all_gather | solution.py:159
  71.0 6.1 gather_fusion
  83.4 37.4 %all-reduce.10 = f32[64,128]{1,0:T(8,128)S(1)} all-reduce(f32[64,128]{1,0:T(8,128)S(1)} %scatter_custom_fusion.4), channel_id=2, replica_groups=mesh['mat'=4,'frac'=8] {'frac'}, use_global_device_ids=true, to_apply=%region_9.10.clone | all-reduce | flops 8192 | bytes 65536
  138.0 40.6 %psum.98 = f32[8192]{0:T(1024)S(1)} all-reduce(f32[8192]{0:T(1024)S(1)} %scatter_custom_fusion.3), channel_id=1, replica_groups=mesh['mat'=4,'frac'=8] {'mat','frac'}, use_global_device_ids=true, to_apply=%region_7.8 | all-reduce | flops 8192 | bytes 65536 | tf_op jit(solution)/shard_map/psum | solution.py:162
  178.7 31.1 %all_gather.27 = f32[8192]{0:T(1024)S(1)} all-gather(f32[1024]{0:T(1024)S(1)} %fusion.134), channel_id=1, replica_groups=mesh['mat'=4,'frac'=8] {'frac'}, dimensions={0}, use_global_device_ids=true | all-gather | bytes 36864 | tf_op jit(solution)/shard_map/all_gather | solution.py:116
  214.0 36.8 %all-reduce.11 = f32[64,128]{1,0:T(8,128)S(1)} all-reduce(f32[64,128]{1,0:T(8,128)S(1)} %scatter_custom_fusion.5), channel_id=3, replica_groups=mesh['mat'=4,'frac'=8] {'frac'}, use_global_device_ids=true, to_apply=%region_13.14.clone | all-reduce | flops 8192 | bytes 65536
  251.5 17.8 %all-reduce.23 = (f32[]{:T(128)}, f32[]{:T(128)}) all-reduce(f32[]{:T(128)} %get-tuple-element.38, f32[]{:T(128)} %get-tuple-element.37), channel_id=1, replica_groups=mesh['mat'=4,'frac'=8] {'frac'}, use_global_device_ids=true, to_apply=%region_11.12 | all-reduce | flops 2 | bytes 16 | tf_op jit(solution)/shard_map/psum | solution.py:129
  270.6 30.6 %all_gather.28 = f32[8192]{0:T(1024)S(1)} all-gather(f32[1024]{0:T(1024)S(1)} %multiply_subtract_fusion.3), channel_id=1, replica_groups=mesh['mat'=4,'frac'=8] {'frac'}, dimensions={0}, use_global_device_ids=true | all-gather | bytes 36864 | tf_op jit(solution)/shard_map/all_gather | solution.py:116
  305.4 34.9 %all-reduce.12 = f32[64,128]{1,0:T(8,128)S(1)} all-reduce(f32[64,128]{1,0:T(8,128)S(1)} %scatter_custom_fusion.6), channel_id=4, replica_groups=mesh['mat'=4,'frac'=8] {'frac'}, use_global_device_ids=true, to_apply=%region_19.20.clone | all-reduce | flops 8192 | bytes 65536
  341.0 17.8 %all-reduce.22 = (f32[]{:T(128)}, f32[]{:T(128)}) all-reduce(f32[]{:T(128)} %get-tuple-element.36, f32[]{:T(128)} %get-tuple-element.35), channel_id=1, replica_groups=mesh['mat'=4,'frac'=8] {'frac'}, use_global_device_ids=true, to_apply=%region_17.18 | all-reduce | flops 2 | bytes 16 | tf_op jit(solution)/shard_map/psum | solution.py:129
  363.2 30.6 %all_gather.29 = f32[8192]{0:T(1024)S(1)} all-gather(f32[1024]{0:T(1024)S(1)} %multiply_subtract_fusion.2), channel_id=1, replica_groups=mesh['mat'=4,'frac'=8] {'frac'}, dimensions={0}, use_global_device_ids=true | all-gather | bytes 36864 | tf_op jit(solution)/shard_map/all_gather | solution.py:116
  398.0 34.9 %all-reduce.13 = f32[64,128]{1,0:T(8,128)S(1)} all-reduce(f32[64,128]{1,0:T(8,128)S(1)} %scatter_custom_fusion.7), channel_id=5, replica_groups=mesh['mat'=4,'frac'=8] {'frac'}, use_global_device_ids=true, to_apply=%region_25.26.clone | all-reduce | flops 8192 | bytes 65536
  433.6 17.8 %all-reduce.21 = (f32[]{:T(128)}, f32[]{:T(128)}) all-reduce(f32[]{:T(128)} %get-tuple-element.34, f32[]{:T(128)} %get-tuple-element.33), channel_id=1, replica_groups=mesh['mat'=4,'frac'=8] {'frac'}, use_global_device_ids=true, to_apply=%region_23.24 | all-reduce | flops 2 | bytes 16 | tf_op jit(solution)/shard_map/psum | solution.py:129
  455.1 30.6 %all_gather.30 = f32[8192]{0:T(1024)S(1)} all-gather(f32[1024]{0:T(1024)S(1)} %multiply_add_fusion.1), channel_id=1, replica_groups=mesh['mat'=4,'frac'=8] {'frac'}, dimensions={0}, use_global_device_ids=true | all-gather | bytes 36864 | tf_op jit(solution)/shard_map/all_gather | solution.py:159
  487.1 7.8 scatter_custom_fusion.2
  506.2 7.6 broadcast_select_fusion.1
  531.1 37.2 %all-reduce.14 = f32[64,128]{1,0:T(8,128)S(1)} all-reduce(f32[64,128]{1,0:T(8,128)S(1)} %scatter_custom_fusion.11), channel_id=6, replica_groups=mesh['mat'=4,'frac'=8] {'frac'}, use_global_device_ids=true, to_apply=%region_33.34.clone | all-reduce | flops 8192 | bytes 65536
  568.3 8.4 fusion.75
  578.2 6.2 gather_fusion.3
  609.2 40.8 %psum.105 = f32[8192]{0:T(1024)S(1)} all-reduce(f32[8192]{0:T(1024)S(1)} %scatter_custom_fusion.10), channel_id=1, replica_groups=mesh['mat'=4,'frac'=8] {'mat','frac'}, use_global_device_ids=true, to_apply=%region_31.32 | all-reduce | flops 8192 | bytes 65536 | tf_op jit(solution)/shard_map/psum | solution.py:162
  650.1 30.6 %all_gather.31 = f32[8192]{0:T(1024)S(1)} all-gather(f32[1024]{0:T(1024)S(1)} %fusion.119), channel_id=1, replica_groups=mesh['mat'=4,'frac'=8] {'frac'}, dimensions={0}, use_global_device_ids=true | all-gather | bytes 36864 | tf_op jit(solution)/shard_map/all_gather | solution.py:116
  685.1 36.9 %all-reduce.15 = f32[64,128]{1,0:T(8,128)S(1)} all-reduce(f32[64,128]{1,0:T(8,128)S(1)} %scatter_custom_fusion.12), channel_id=7, replica_groups=mesh['mat'=4,'frac'=8] {'frac'}, use_global_device_ids=true, to_apply=%region_37.38.clone | all-reduce | flops 8192 | bytes 65536
  722.6 17.8 %all-reduce.20 = (f32[]{:T(128)}, f32[]{:T(128)}) all-reduce(f32[]{:T(128)} %get-tuple-element.32, f32[]{:T(128)} %get-tuple-element.31), channel_id=1, replica_groups=mesh['mat'=4,'frac'=8] {'frac'}, use_global_device_ids=true, to_apply=%region_35.36 | all-reduce | flops 2 | bytes 16 | tf_op jit(solution)/shard_map/psum | solution.py:129
  741.7 30.6 %all_gather.32 = f32[8192]{0:T(1024)S(1)} all-gather(f32[1024]{0:T(1024)S(1)} %multiply_subtract_fusion.1), channel_id=1, replica_groups=mesh['mat'=4,'frac'=8] {'frac'}, dimensions={0}, use_global_device_ids=true | all-gather | bytes 36864 | tf_op jit(solution)/shard_map/all_gather | solution.py:116
  776.7 34.9 %all-reduce.16 = f32[64,128]{1,0:T(8,128)S(1)} all-reduce(f32[64,128]{1,0:T(8,128)S(1)} %scatter_custom_fusion.13), channel_id=8, replica_groups=mesh['mat'=4,'frac'=8] {'frac'}, use_global_device_ids=true, to_apply=%region_43.44.clone | all-reduce | flops 8192 | bytes 65536
  812.2 17.8 %all-reduce.19 = (f32[]{:T(128)}, f32[]{:T(128)}) all-reduce(f32[]{:T(128)} %get-tuple-element.30, f32[]{:T(128)} %get-tuple-element.29), channel_id=1, replica_groups=mesh['mat'=4,'frac'=8] {'frac'}, use_global_device_ids=true, to_apply=%region_41.42 | all-reduce | flops 2 | bytes 16 | tf_op jit(solution)/shard_map/psum | solution.py:129
  834.8 30.6 %all_gather.33 = f32[8192]{0:T(1024)S(1)} all-gather(f32[1024]{0:T(1024)S(1)} %multiply_subtract_fusion), channel_id=1, replica_groups=mesh['mat'=4,'frac'=8] {'frac'}, dimensions={0}, use_global_device_ids=true | all-gather | bytes 36864 | tf_op jit(solution)/shard_map/all_gather | solution.py:116
  872.5 38.1 %all-reduce.17 = f32[64,128]{1,0:T(8,128)S(1)} all-reduce(f32[64,128]{1,0:T(8,128)S(1)} %scatter_custom_fusion.14), channel_id=9, replica_groups=mesh['mat'=4,'frac'=8] {'frac'}, use_global_device_ids=true, to_apply=%region_49.50.clone | all-reduce | flops 8192 | bytes 65536
  911.4 8.3 scatter_custom_fusion.9
  922.2 8.4 broadcast_select_fusion
  936.7 17.8 %all-reduce.18 = (f32[]{:T(128)}, f32[]{:T(128)}) all-reduce(f32[]{:T(128)} %get-tuple-element.28, f32[]{:T(128)} %get-tuple-element.27), channel_id=1, replica_groups=mesh['mat'=4,'frac'=8] {'frac'}, use_global_device_ids=true, to_apply=%region_47.48 | all-reduce | flops 2 | bytes 16 | tf_op jit(solution)/shard_map/psum | solution.py:129
  969.1 9.4 fusion.74
  (221 shorter events, 169.4 us)
Async XLA Ops:
  0.6 64.4 %copy-start.15 = (f32[1024]{0:T(1024)S(1)}, f32[1024]{0:T(1024)}, u32[]{:S(2)}) copy-start(f32[1024]{0:T(1024)} %param.29) | copy-start | bytes 12292
  2.3 499.2 %collective-permute-start = (f32[64,256]{1,0:T(8,128)}, f32[64,256]{1,0:T(8,128)S(1)}, u32[]{:S(2)}, u32[]{:S(2)}) collective-permute-start(f32[64,256]{1,0:T(8,128)} %slice_bitcast_fusion.7), channel_id=1, source_target_pairs={{0,8},{8,16},{16,24},{1,9},{9,17},{17,25},{2,10},{10,18},{18,26},{... | collective-permute-start | bytes 196616 | tf_op jit(solution)/shard_map/ppermute | solution.py:17
  5.7 480.6 %collective-permute-start.1 = (f32[16,256]{1,0:T(8,128)S(1)}, f32[16,256]{1,0:T(8,128)S(1)}, u32[]{:S(2)}, u32[]{:S(2)}) collective-permute-start(f32[16,256]{1,0:T(8,128)S(1)} %bitcast.415), channel_id=1, source_target_pairs={{0,1},{1,2},{2,3},{3,4},{4,5},{5,6},{6,7},{8,9},{9,10},{10,11},{11... | collective-permute-start | bytes 49160 | tf_op jit(solution)/shard_map/ppermute | solution.py:17
  11.5 486.0 %collective-permute-start.3 = (f32[1,64,256]{2,1,0:T(8,128)}, f32[1,64,256]{2,1,0:T(8,128)S(1)}, u32[]{:S(2)}, u32[]{:S(2)}) collective-permute-start(f32[1,64,256]{2,1,0:T(8,128)} %get-tuple-element.72), channel_id=1, source_target_pairs={{0,8},{8,16},{16,24},{1,9},{9,17},{17,25},{2,10},{10,18},{18,26},{... | collective-permute-start | bytes 196616 | tf_op jit(solution)/shard_map/ppermute | solution.py:25
  14.9 482.8 %collective-permute-start.2 = (f32[1,64,256]{2,1,0:T(8,128)}, f32[1,64,256]{2,1,0:T(8,128)S(1)}, u32[]{:S(2)}, u32[]{:S(2)}) collective-permute-start(f32[1,64,256]{2,1,0:T(8,128)} %get-tuple-element.71), channel_id=1, source_target_pairs={{8,0},{16,8},{24,16},{9,1},{17,9},{25,17},{10,2},{18,10},{26,18},{... | collective-permute-start | bytes 196616 | tf_op jit(solution)/shard_map/ppermute | solution.py:28
  19.8 109.1 %copy-start.20 = (s32[512,1]{0,1:T(1,128)}, s32[512,1]{0,1:T(1,128)S(1)}, u32[]{:S(2)}) copy-start(s32[512,1]{0,1:T(1,128)S(1)} %compare_select_fusion.1) | copy-start | bytes 6148
  23.1 47.8 %all-to-all-start = ((s32[32,1,32]{2,1,0:T(1,128)}), s32[32,1,32]{2,1,0:T(1,128)S(1)}, u32[]{:S(2)}, u32[]{:S(2)}) async-start(s32[32,1,32]{2,1,0:T(1,128)} %all_to_all.30), calls=%async_computation | async-start | bytes 32768 | tf_op jit(solution)/shard_map/all_to_all | solution.py:112
  29.0 97.5 %copy-start.18 = (s32[1024]{0:T(1024)}, s32[1024]{0:T(1024)S(1)}, u32[]{:S(2)}) copy-start(s32[1024]{0:T(1024)S(1)} %pad_clamp_fusion.2) | copy-start | bytes 12292
  62.6 334.8 %copy-start.25 = (s32[32]{0:T(128)}, s32[32]{0:T(128)S(1)}, u32[]{:S(2)}) copy-start(s32[32]{0:T(128)S(1)} %fusion.141) | copy-start | bytes 388
  77.9 47.4 %all-to-all-start.1 = ((f32[32,1,32]{2,1,0:T(1,128)}), f32[32,1,32]{2,1,0:T(1,128)S(1)}, u32[]{:S(2)}, u32[]{:S(2)}) async-start(f32[32,1,32]{2,1,0:T(1,128)} %all_to_all.32), calls=%async_computation.1 | async-start | bytes 32768 | tf_op jit(solution)/shard_map/all_to_all | solution.py:155
  125.3 361.8 %copy-start.23 = (s32[1024]{0:T(1024)}, s32[1024]{0:T(1024)S(1)}, u32[]{:S(2)}) copy-start(s32[1024]{0:T(1024)S(1)} %reshape.528) | copy-start | bytes 12292
  135.5 350.9 %all-to-all-start.2 = ((f32[32,1,32]{2,1,0:T(1,128)}), f32[32,1,32]{2,1,0:T(1,128)S(1)}, u32[]{:S(2)}, u32[]{:S(2)}) async-start(f32[32,1,32]{2,1,0:T(1,128)} %all_to_all.34), calls=%async_computation.2 | async-start | bytes 32768 | tf_op jit(solution)/shard_map/all_to_all | solution.py:171
  397.3 100.2 %copy-start.8 = (f32[16,64,256]{2,1,0:T(8,128)S(1)}, f32[16,64,256]{2,1,0:T(8,128)}, u32[]{:S(2)}) copy-start(f32[16,64,256]{2,1,0:T(8,128)} %param.17) | copy-start | bytes 3145732
  498.7 7.4 collective-permute-start.5
  500.2 5.9 collective-permute-start.4
  513.9 6.2 collective-permute-start.6
  515.2 4.9 collective-permute-start.7
  520.1 48.2 %collective-permute-start.9 = (f32[18,1,256]{2,1,0:T(1,128)S(1)}, f32[18,1,256]{2,1,0:T(1,128)S(1)}, u32[]{:S(2)}, u32[]{:S(2)}) collective-permute-start(f32[18,1,256]{2,1,0:T(1,128)S(1)} %get-tuple-element.62), channel_id=1, source_target_pairs={{0,1},{1,2},{2,3},{3,4},{4,5},{5,6},{6,7},{8,9},{9,10},{10,11},{11... | collective-permute-start | bytes 55304 | tf_op jit(solution)/shard_map/ppermute | solution.py:25
  524.7 43.6 %collective-permute-start.8 = (f32[18,1,256]{2,1,0:T(1,128)S(1)}, f32[18,1,256]{2,1,0:T(1,128)S(1)}, u32[]{:S(2)}, u32[]{:S(2)}) collective-permute-start(f32[18,1,256]{2,1,0:T(1,128)S(1)} %get-tuple-element.61), channel_id=1, source_target_pairs={{1,0},{2,1},{3,2},{4,3},{5,4},{6,5},{7,6},{9,8},{10,9},{11,10},{12... | collective-permute-start | bytes 55304 | tf_op jit(solution)/shard_map/ppermute | solution.py:28
  584.4 65.7 %copy-start.17 = (f32[1024]{0:T(1024)S(1)}, f32[1024]{0:T(1024)}, u32[]{:S(2)}) copy-start(f32[1024]{0:T(1024)} %param.28) | copy-start | bytes 12292
  585.1 10.4 %all-to-all-start.3 = ((f32[32,1,32]{2,1,0:T(1,128)}), f32[32,1,32]{2,1,0:T(1,128)S(1)}, u32[]{:S(2)}, u32[]{:S(2)}) async-start(f32[32,1,32]{2,1,0:T(1,128)} %all_to_all.36), calls=%async_computation.3 | async-start | bytes 32768 | tf_op jit(solution)/shard_map/all_to_all | solution.py:155
  589.2 278.6 %collective-permute-start.10 = (f32[1,64,256]{2,1,0:T(8,128)S(1)}, f32[1,64,256]{2,1,0:T(8,128)S(1)}, u32[]{:S(2)}, u32[]{:S(2)}) collective-permute-start(f32[1,64,256]{2,1,0:T(8,128)S(1)} %get-tuple-element.68), channel_id=1, source_target_pairs={{8,0},{16,8},{24,16},{9,1},{17,9},{25,17},{10,2},{18,10},{26,18},{... | collective-permute-start | bytes 196616 | tf_op jit(solution)/shard_map/ppermute | solution.py:28
  590.5 277.3 %collective-permute-start.11 = (f32[1,64,256]{2,1,0:T(8,128)S(1)}, f32[1,64,256]{2,1,0:T(8,128)S(1)}, u32[]{:S(2)}, u32[]{:S(2)}) collective-permute-start(f32[1,64,256]{2,1,0:T(8,128)S(1)} %get-tuple-element.67), channel_id=1, source_target_pairs={{0,8},{8,16},{16,24},{1,9},{9,17},{17,25},{2,10},{10,18},{18,26},{... | collective-permute-start | bytes 196616 | tf_op jit(solution)/shard_map/ppermute | solution.py:25
  598.5 85.7 %copy-start.24 = (f32[512]{0:T(512)}, f32[512]{0:T(512)S(1)}, u32[]{:S(2)}) copy-start(f32[512]{0:T(512)S(1)} %subtract_multiply_fusion) | copy-start | bytes 6148
  605.2 305.4 %all-to-all-start.4 = ((f32[32,1,32]{2,1,0:T(1,128)}), f32[32,1,32]{2,1,0:T(1,128)S(1)}, u32[]{:S(2)}, u32[]{:S(2)}) async-start(f32[32,1,32]{2,1,0:T(1,128)} %all_to_all.38), calls=%async_computation.4 | async-start | bytes 32768 | tf_op jit(solution)/shard_map/all_to_all | solution.py:171
  774.7 93.1 %copy-start.4 = (f32[16,64,256]{2,1,0:T(8,128)S(1)}, f32[16,64,256]{2,1,0:T(8,128)}, u32[]{:S(2)}) copy-start(f32[16,64,256]{2,1,0:T(8,128)} %copy-done.3) | copy-start | bytes 3145732
  867.9 54.3 %collective-permute-start.13 = (f32[18,1,256]{2,1,0:T(1,128)S(1)}, f32[18,1,256]{2,1,0:T(1,128)S(1)}, u32[]{:S(2)}, u32[]{:S(2)}) collective-permute-start(f32[18,1,256]{2,1,0:T(1,128)S(1)} %get-tuple-element.60), channel_id=1, source_target_pairs={{0,1},{1,2},{2,3},{3,4},{4,5},{5,6},{6,7},{8,9},{9,10},{10,11},{11... | collective-permute-start | bytes 55304 | tf_op jit(solution)/shard_map/ppermute | solution.py:25
  869.2 53.0 %collective-permute-start.12 = (f32[18,1,256]{2,1,0:T(1,128)S(1)}, f32[18,1,256]{2,1,0:T(1,128)S(1)}, u32[]{:S(2)}, u32[]{:S(2)}) collective-permute-start(f32[18,1,256]{2,1,0:T(1,128)S(1)} %get-tuple-element.59), channel_id=1, source_target_pairs={{1,0},{2,1},{3,2},{4,3},{5,4},{6,5},{7,6},{9,8},{10,9},{11,10},{12... | collective-permute-start | bytes 55304 | tf_op jit(solution)/shard_map/ppermute | solution.py:28
  931.7 26.8 %collective-permute-start.14 = (f32[1,64,256]{2,1,0:T(8,128)S(1)}, f32[1,64,256]{2,1,0:T(8,128)S(1)}, u32[]{:S(2)}, u32[]{:S(2)}) collective-permute-start(f32[1,64,256]{2,1,0:T(8,128)S(1)} %get-tuple-element.66), channel_id=1, source_target_pairs={{8,0},{16,8},{24,16},{9,1},{17,9},{25,17},{10,2},{18,10},{26,18},{... | collective-permute-start | bytes 196616 | tf_op jit(solution)/shard_map/ppermute | solution.py:28
  933.0 25.5 %collective-permute-start.15 = (f32[1,64,256]{2,1,0:T(8,128)S(1)}, f32[1,64,256]{2,1,0:T(8,128)S(1)}, u32[]{:S(2)}, u32[]{:S(2)}) collective-permute-start(f32[1,64,256]{2,1,0:T(8,128)S(1)} %get-tuple-element.65), channel_id=1, source_target_pairs={{0,8},{8,16},{16,24},{1,9},{9,17},{17,25},{2,10},{10,18},{18,26},{... | collective-permute-start | bytes 196616 | tf_op jit(solution)/shard_map/ppermute | solution.py:25
  959.5 5.8 collective-permute-start.17
  963.4 5.7 collective-permute-start.16
  (18 other events, 460.2 us)
where the time goes:
time: 988 us; the launch traced here: 979 us
  blocking collectives  725 us (73%)
  other arithmetic  79.7 us (8%)
  starting transfers between devices  61.8 us (6%)
  local copies, waits for them, and re-layouts  60.8 us (6%)
  matrix products  23.6 us (2%)
  between operations  22.3 us (2%)
    unnamed x8, blocking collectives  291 us
    all_gather x6, blocking collectives, fracture_apply(): whole = lax.all_gather(vector, 'frac', axis=0, tiled=True)  184 us
    psum x6, blocking collectives, two_products(): lax.psum((jnp.sum(residual * residual), jnp.sum(residual * image)), 'frac')  107 us
    psum x2, blocking collectives, body(): summed = lax.psum(landed, ('mat', 'frac'))  81.4 us
    all_gather x2, blocking collectives, body(): fracture_whole = lax.all_gather(fracture, 'frac', axis=0, tiled=True)  61.7 us
    select_n x4, other arithmetic, relax(): return jnp.where(inside, updated, 0.0)  33.9 us
    ppermute x8, starting transfers between devices, with_halo(): lax.ppermute(lax.slice_in_dim(block, block.shape[dim] - width, None, axis...  23.7 us
  transfers between devices with their start and end apart: 23, of which 2 were waited for; matrix products, arithmetic and copies ran while one was open for 12% of the time, Pallas kernels for 0%

commit v1 on v0

v1 whole, which is shorter than its diff:
```python
import functools

import jax
import jax.numpy as jnp
from jax import lax
from jax.experimental import pallas as pl
from jax.experimental.pallas import tpu as pltpu
from jax.sharding import PartitionSpec as P

SWEEPS = 2
CG_ITERS = 3
OUTER = 2

EXACT = lax.Precision.HIGHEST
MESH = pl.DeviceIdType.MESH

relax_weight = 0.8


def shifted(value, axis, steps):
    count = lax.axis_size(axis)
    leading, last = (max(0, -steps), min(count, count - steps))
    return lax.ppermute(value, axis, [(source, source + steps) for source in range(leading, last)])


def with_halo(block, sides, width):
    for axis, dim in sides:
        count = lax.axis_size(axis)
        forward = [(i, i + 1) for i in range(count - 1)]
        backward = [(target, source) for source, target in forward]
        low = lax.ppermute(
            lax.slice_in_dim(block, block.shape[dim] - width, None, axis=dim), axis, forward
        )
        high = lax.ppermute(lax.slice_in_dim(block, 0, width, axis=dim), axis, backward)
        block = jnp.concatenate([low, block, high], axis=dim)
    return block


def shift_next(values, along):
    padding = [(0, 0)] * values.ndim
    padding[along] = (0, 1)
    return lax.slice_in_dim(jnp.pad(values, padding), 1, values.shape[along] + 1, axis=along)


def shift_prev(values, along):
    padding = [(0, 0)] * values.ndim
    padding[along] = (1, 0)
    return lax.slice_in_dim(jnp.pad(values, padding), 0, values.shape[along], axis=along)


def relax(padded, coef_part, source_part, inside):
    centre = padded[1:-1, 1:-1]
    tx_here = coef_part[0, 1:-1, 1:-1]
    tx_low = coef_part[0, :-2, 1:-1]
    ty_here = coef_part[1, 1:-1, 1:-1]
    ty_low = coef_part[1, 1:-1, :-2]
    tz_here = coef_part[2, 1:-1, 1:-1]
    tz_low = shift_prev(tz_here, 2)
    cell_part = coef_part[3, 1:-1, 1:-1]
    base_part = coef_part[4, 1:-1, 1:-1]
    diagonal = cell_part + tx_here + tx_low + ty_here + ty_low + tz_here + tz_low
    diagonal = jnp.where(inside, diagonal, 1.0)
    applied = (
        diagonal * centre
        - tx_here * padded[2:, 1:-1]
        - tx_low * padded[:-2, 1:-1]
        - ty_here * padded[1:-1, 2:]
        - ty_low * padded[1:-1, :-2]
        - tz_here * shift_next(centre, 2)
        - tz_low * shift_prev(centre, 2)
    )
    updated = centre + relax_weight * (base_part + source_part - applied) / diagonal
    return jnp.where(inside, updated, 0.0)


def fracture_kernel(first, n_frac, n_mat, *refs):
    if first:
        (trace_ref, kappa_ref, place_ref, tiles_ref, cols_ref, cols_row_ref, diag_ref, begin_ref, source_ref,
         flux_ref, full_ref, resid_ref, load_ref, *scratch) = refs
    else:
        (trace_ref, kappa_ref, place_ref, tiles_ref, cols_ref, cols_row_ref, diag_ref, begin_ref, before_ref, loaded_ref,
         flux_ref, own_ref, *scratch) = refs
    gather_ref, outgo_ref, income_ref, mat_ref, back_ref, forth_ref, sems = *scratch[:6], scratch[6:]
    gather_send, gather_recv, part_send, part_recv, mat_send, mat_recv = sems
    rows, tiles_row = tiles_ref.shape[0], tiles_ref.shape[1]
    size_b = tiles_ref.shape[3]
    blocks = rows * n_frac
    me = lax.axis_index("frac")
    me_mat = lax.axis_index("mat")
    mine = pl.ds(pl.multiple_of(me * rows, rows), rows)

    barrier = pltpu.get_barrier_semaphore()
    for k in range(1, n_frac):
        pl.semaphore_signal(barrier, inc=1, device_id={"frac": lax.rem(me + k, n_frac)}, device_id_type=MESH)
    for k in range(1, n_mat):
        pl.semaphore_signal(barrier, inc=1, device_id={"mat": lax.rem(me_mat + k, n_mat)}, device_id_type=MESH)
    pl.semaphore_wait(barrier, n_frac + n_mat - 2)

    sent = []

    def gather(phase, value):
        gather_ref[phase, mine, :] = value
        copies = []
        for k in range(1, n_frac):
            copy = pltpu.make_async_remote_copy(
                src_ref=gather_ref.at[phase, mine],
                dst_ref=gather_ref.at[phase, mine],
                send_sem=gather_send.at[phase, k - 1],
                recv_sem=gather_recv.at[phase, k - 1],
                device_id={"frac": lax.rem(me + k, n_frac)},
                device_id_type=MESH,
            )
            copy.start()
            copies.append(copy)
        sent.extend(copies)
        return copies

    def exchange(phase, low, high):
        part = pl.ds(low, high - low)
        copies = []
        for k in range(1, n_frac):
            target = lax.rem(me + k, n_frac)
            copy = pltpu.make_async_remote_copy(
                src_ref=outgo_ref.at[phase, target, part],
                dst_ref=income_ref.at[phase, me, part],
                send_sem=part_send.at[phase, k - 1],
                recv_sem=part_recv.at[phase, k - 1],
                device_id={"frac": target},
                device_id_type=MESH,
            )
            copy.start()
            copies.append(copy)
        sent.extend(copies)
        income_ref[phase, me, part, :] = outgo_ref[phase, me, part, :]
        for copy in copies:
            copy.wait_recv()
        total = income_ref[phase, 0, part, :]
        for k in range(1, n_frac):
            total = total + income_ref[phase, k, part, :]
        return total

    def products(phase, with_back):
        def row(r, carry):
            across = gather_ref[phase, pl.ds(me * rows + r, 1), :]
            down = jnp.broadcast_to(across, (size_b, size_b)).T
            total = jnp.zeros((size_b, size_b), jnp.float32)
            for t in range(tiles_row):
                tile = tiles_ref[r, t]
                total = total + tile * gather_ref[phase, pl.ds(cols_ref[r, t], 1), :]
                if with_back:
                    back_ref[pl.ds(r * tiles_row + t, 1), :] = jnp.sum(tile * down, axis=0, keepdims=True)
            forth_ref[pl.ds(r, 1), :] = jnp.sum(total.T, axis=0, keepdims=True)
            return carry

        lax.fori_loop(0, rows, row, 0)
        forward = forth_ref[...]
        if not with_back:
            return forward, None
        named = lax.broadcasted_iota(jnp.int32, (blocks, rows * tiles_row), 0) == cols_row_ref[...]
        spread = jnp.dot(named.astype(jnp.float32), back_ref[...], precision=EXACT, preferred_element_type=jnp.float32)
        return forward, spread

    def total_of(values):
        return jnp.sum(values, axis=(0, 1), keepdims=True)

    diag = diag_ref[...]
    place = place_ref[...]
    slots = place.shape[1]
    block_of = place // size_b
    lane_of = place - block_of * size_b
    by_block = (lax.broadcasted_iota(jnp.int32, (blocks, slots), 0) == block_of).astype(jnp.float32)
    by_lane = (lax.broadcasted_iota(jnp.int32, (size_b, slots), 0) == lane_of).astype(jnp.float32)

    def fluxes(full):
        picked = lax.dot_general(full, by_block, (((0,), (0,)), ((), ())), precision=EXACT, preferred_element_type=jnp.float32)
        at_slots = jnp.sum(picked * by_lane, axis=0, keepdims=True)
        flux = kappa_ref[...] * (trace_ref[...] - at_slots)
        flux_ref[...] = flux
        return lax.dot_general(by_block * flux, by_lane, (((1,), (1,)), ((), ())), precision=EXACT, preferred_element_type=jnp.float32)

    if first:
        begin = begin_ref[...]
        for copy in gather(0, begin):
            copy.wait_recv()
        fracture = gather_ref[0]
        landed = fluxes(fracture)
        forward, spread = products(0, True)
        for k in range(n_frac):
            outgo_ref[0, k, 0:rows, :] = spread[k * rows : (k + 1) * rows]
            outgo_ref[0, k, rows : 2 * rows, :] = landed[k * rows : (k + 1) * rows]
        both = exchange(0, 0, 2 * rows)
        image = diag * begin + 0.5 * (forward + both[0:rows])
        part_load = both[rows : 2 * rows]
    else:
        fracture = begin_ref[...]
        landed = fluxes(fracture)
        for k in range(n_frac):
            outgo_ref[0, k, rows : 2 * rows, :] = landed[k * rows : (k + 1) * rows]
        part_load = exchange(0, rows, 2 * rows)
    mat_ref[me_mat] = part_load
    copies = []
    for k in range(1, n_mat):
        copy = pltpu.make_async_remote_copy(
            src_ref=mat_ref.at[me_mat],
            dst_ref=mat_ref.at[me_mat],
            send_sem=mat_send.at[k - 1],
            recv_sem=mat_recv.at[k - 1],
            device_id={"mat": lax.rem(me_mat + k, n_mat)},
            device_id_type=MESH,
        )
        copy.start()
        copies.append(copy)
    sent.extend(copies)
    for copy in copies:
        copy.wait_recv()
    load = mat_ref[0]
    for k in range(1, n_mat):
        load = load + mat_ref[k]
    if first:
        load_ref[...] = load
        residual = source_ref[...] + load - image
    else:
        residual = before_ref[...] + (load - loaded_ref[...])

    for step in range(CG_ITERS):
        phase = step + 1
        needed = first or step + 1 < CG_ITERS
        for copy in gather(phase, residual):
            copy.wait_recv()
        whole = gather_ref[phase]
        forward, spread = products(phase, needed)
        inner = residual * (diag * residual + forward)
        for k in range(n_frac):
            if needed:
                outgo_ref[phase, k, 0:rows, :] = spread[k * rows : (k + 1) * rows]
            outgo_ref[phase, k, rows : 2 * rows, :] = inner
        both = exchange(phase, 0 if needed else rows, 2 * rows)
        if needed:
            image = diag * residual + 0.5 * (forward + both[0:rows])
            product = total_of(both[rows : 2 * rows])
        else:
            product = total_of(both)
        norm_next = total_of(whole * whole)
        if step == 0:
            alpha = norm_next / product
            direction = whole
            along = image
        else:
            ratio = norm_next / norm_now
            alpha = norm_next / (product - ratio * norm_next / alpha)
            direction = whole + ratio * direction
            if needed:
                along = image + ratio * along
        norm_now = norm_next
        fracture = fracture + alpha * direction
        if needed:
            residual = residual - alpha * along
    if first:
        full_ref[...] = fracture
        resid_ref[...] = residual
    else:
        gather_ref[0] = fracture
        own_ref[...] = gather_ref[0, mine, :]
    for copy in sent:
        copy.wait_send()


def fracture_step(first, trace, kappa, place, tiles, tile_cols, diag, *extra):
    n_frac, n_mat = lax.axis_size("frac"), lax.axis_size("mat")
    rows, tiles_row, size_b = tiles.shape[0], tiles.shape[1], tiles.shape[3]
    blocks = rows * n_frac
    own = jax.ShapeDtypeStruct((rows, size_b), jnp.float32)
    full = jax.ShapeDtypeStruct((blocks, size_b), jnp.float32)
    vmem = pl.BlockSpec(memory_space=pltpu.VMEM)
    smem = pl.BlockSpec(memory_space=pltpu.SMEM)
    phases = CG_ITERS + 1
    outs = (trace_shape(trace), full, own, own) if first else (trace_shape(trace), own)
    return pl.pallas_call(
        functools.partial(fracture_kernel, first, n_frac, n_mat),
        out_shape=outs,
        in_specs=[vmem] * 4 + [smem] + [vmem] * (2 + len(extra)),
        out_specs=(vmem,) * len(outs),
        scratch_shapes=[
            pltpu.VMEM((phases, blocks, size_b), jnp.float32),
            pltpu.VMEM((phases, n_frac, 2 * rows, size_b), jnp.float32),
            pltpu.VMEM((phases, n_frac, 2 * rows, size_b), jnp.float32),
            pltpu.VMEM((n_mat, rows, size_b), jnp.float32),
            pltpu.VMEM((rows * tiles_row, size_b), jnp.float32),
            pltpu.VMEM((rows, size_b), jnp.float32),
            pltpu.SemaphoreType.DMA((phases, n_frac - 1)),
            pltpu.SemaphoreType.DMA((phases, n_frac - 1)),
            pltpu.SemaphoreType.DMA((phases, n_frac - 1)),
            pltpu.SemaphoreType.DMA((phases, n_frac - 1)),
            pltpu.SemaphoreType.DMA((n_mat - 1,)),
            pltpu.SemaphoreType.DMA((n_mat - 1,)),
        ],
        compiler_params=pltpu.CompilerParams(collective_id=0 if first else 1, has_side_effects=True),
        name="fracture_first" if first else "fracture_next",
    )(trace, kappa, place, tiles, tile_cols, tile_cols.reshape(1, -1), diag, *extra)


def trace_shape(trace):
    return jax.ShapeDtypeStruct(trace.shape, jnp.float32)


def body(
    pressure_start,
    face_trans,
    cell_coef,
    matrix_source,
    mortar_owner,
    mortar_cell,
    mortar_frac,
    mortar_kappa,
    tiles,
    tile_cols,
    frac_diag,
    frac_source,
    fracture_start,
):
    width_x, width_y, depth_z = pressure_start.shape
    cells = width_x * width_y * depth_z
    mat_count = lax.axis_size("mat")
    frac_count = lax.axis_size("frac")
    devices = mat_count * frac_count
    row_mat = lax.axis_index("mat")
    row_frac = lax.axis_index("frac")
    size_b = tiles.shape[2]
    coefs = jnp.concatenate([face_trans, cell_coef[None], matrix_source[None]], 0)
    lower_x = shifted(face_trans[0, -1], "mat", 1)
    lower_y = shifted(face_trans[1, :, -1], "frac", 1)
    coef_ext = jnp.pad(coefs, ((0, 0), (1, 1), (1, 1), (0, 0)))
    coef_ext = coef_ext.at[0, 0, 1:-1].set(lower_x)
    coef_ext = coef_ext.at[1, 1:-1, 0].set(lower_y)
    owner = mortar_owner[:, 0]
    mortar_count = owner.shape[0]
    capacity = max(2, 2 * mortar_count // devices)
    hits = (owner[:, None] == jnp.arange(devices, dtype=jnp.int32)[None, :]).astype(jnp.int32)
    ranks = jnp.cumsum(hits, axis=0)
    slot = jnp.sum(ranks * hits, axis=1) - 1
    place = owner * capacity + slot
    slots = devices * capacity
    at_slot = (place[:, None] == jnp.arange(slots, dtype=jnp.int32)[None, :]).astype(jnp.float32)
    payload = jnp.stack([mortar_cell.astype(jnp.float32), mortar_frac.astype(jnp.float32), mortar_kappa])
    outgoing = jnp.dot(payload, at_slot, precision=EXACT).reshape(3, devices, capacity)
    incoming = lax.all_to_all(outgoing, ("mat", "frac"), split_axis=1, concat_axis=1, tiled=True)
    cell_slots = jnp.round(incoming[0]).astype(jnp.int32).reshape(-1)
    frac_slots = jnp.round(incoming[1]).astype(jnp.int32).reshape(1, -1)
    kappa_slots = incoming[2].reshape(1, -1)
    diag = frac_diag.reshape(-1, size_b)
    pressure = pressure_start
    fracture = fracture_start.reshape(-1, size_b)
    global_x = row_mat * width_x - 0 + jnp.arange(width_x)
    global_y = row_frac * width_y - 0 + jnp.arange(width_y)
    inside = (
        ((global_x >= 0) & (global_x < width_x * mat_count))[:, None]
        & ((global_y >= 0) & (global_y < width_y * frac_count))[None, :]
    )[:, :, None]
    for outer_no in range(OUTER):
        trace = pressure.reshape(-1)[cell_slots].reshape(1, -1)
        common = (trace, kappa_slots, frac_slots, tiles, tile_cols, diag)
        if outer_no == 0:
            flux, full, residual, load = fracture_step(True, *common, fracture, frac_source.reshape(-1, size_b))
        else:
            flux, fracture = fracture_step(False, *common, full, residual, load)
        source = jax.ops.segment_sum(flux.reshape(-1), cell_slots, num_segments=cells).reshape(pressure.shape)
        for sweep_no in range(SWEEPS):
            padded = with_halo(pressure, (("mat", 0), ("frac", 1)), 1)
            pressure = relax(padded, coef_ext, source, inside)
    returned = lax.all_to_all(
        flux.reshape(devices, capacity), ("mat", "frac"), split_axis=0, concat_axis=0, tiled=True
    )
    return (pressure, fracture.reshape(-1), returned.reshape(-1)[place])


def solution(mesh):
    in_specs = (
        P("mat", "frac", None),
        P(None, "mat", "frac", None),
        P("mat", "frac", None),
        P("mat", "frac", None),
        P(("mat", "frac"), None),
        P(("mat", "frac")),
        P(("mat", "frac")),
        P(("mat", "frac")),
        P("frac", None, None, None),
        P("frac", None),
        P("frac"),
        P("frac"),
        P("frac"),
    )
    out_specs = (P("mat", "frac", None), P("frac"), P(("mat", "frac")))
    return jax.shard_map(body, mesh=mesh, in_specs=in_specs, out_specs=out_specs, check_vma=False)
```

time: 988 us -> 254 us (0.26)
  blocking collectives: 725 us -> 0 us
  Pallas kernels: 0 us -> 97.1 us
  other arithmetic: 79.7 us -> 47.7 us
  matrix products: 23.6 us -> 1.5 us
  between operations: 22.3 us -> 1.2 us
  local copies, waits for them, and re-layouts: 60.8 us -> 41.6 us
    unnamed x8 -> x0, blocking collectives: 291 us -> none
    all_gather x8 -> x0, blocking collectives: 246 us -> none  [the longest x6 184 us: fracture_apply(): whole = lax.all_gather(vector, 'frac', axis=0, tiled=True)]
    psum x8 -> x0, blocking collectives: 188 us -> none  [the longest x6 107 us: two_products(): lax.psum((jnp.sum(residual * residual), jnp.sum(residual * image)), 'frac')]
    pallas_call x0 -> x2, Pallas kernels: none -> 97.1 us  [fracture_step(): pl.pallas_call(functools.partial(fracture_kernel, first, n_frac, n_mat),...]
    dot_general x16 -> x1, matrix products: 23.6 us -> 1.5 us  [body(): jnp.dot(payload, at_slot, precision=EXACT).reshape(3, devices, capacity)]
    scatter-add x12 -> x2, other arithmetic: 29.3 us -> 14.1 us  [body(): jax.ops.segment_sum(flux.reshape(-1), cell_slots, num_segments=cells)]
    all_to_all x5 -> x2, starting transfers between devices: 21.2 us -> 8.84 us  [the longest x1 5.95 us: body(): lax.all_to_all(outgoing, ('mat', 'frac'), split_axis=1, concat_axis=1, ti...]
    select_n x4, other arithmetic: 33.9 us -> 22.2 us  [relax(): return jnp.where(inside, updated, 0.0)]
  transfers between devices with their start and end apart: 23 -> 20, of which waited for: 2 -> 6; matrix products, arithmetic and copies ran while one was open for 12% -> 26% of each run, Pallas kernels for 0% -> 38%
where the time goes in v1:
time: 254 us; the launch traced here: 253 us
  Pallas kernels  97.1 us (38%)
  starting transfers between devices  54.2 us (21%)
  other arithmetic  47.7 us (19%)
  local copies, waits for them, and re-layouts  41.6 us (16%)
  waiting for transfers between devices  9.8 us (4%)
    pallas_call x2, Pallas kernels, fracture_step(): pl.pallas_call(functools.partial(fracture_kernel, first, n_frac, n_mat),...  97.1 us
    ppermute x8, starting transfers between devices, with_halo(): lax.ppermute(lax.slice_in_dim(block, block.shape[dim] - width, None, axis...  28.2 us
    select_n x4, other arithmetic, relax(): return jnp.where(inside, updated, 0.0)  22.2 us
    gather x2, local copies, waits for them, and re-layouts, body(): trace = pressure.reshape(-1)[cell_slots].reshape(1, -1)  21.1 us
    scatter-add x2, other arithmetic, body(): jax.ops.segment_sum(flux.reshape(-1), cell_slots, num_segments=cells)  14.1 us
    ppermute x8, starting transfers between devices, with_halo(): lax.ppermute(lax.slice_in_dim(block, 0, width, axis=dim), axis, backward)  10.6 us
    ppermute x2, starting transfers between devices, shifted(): lax.ppermute(value, axis, [(source, source + steps) for source in range(l...  6.63 us
    all_to_all x1, starting transfers between devices, body(): lax.all_to_all(outgoing, ('mat', 'frac'), split_axis=1, concat_axis=1, ti...  5.95 us
  transfers between devices with their start and end apart: 20, of which 6 were waited for; matrix products, arithmetic and copies ran while one was open for 26% of the time, Pallas kernels for 38%

profile of v1, /device:TPU:0, one launch (start us, length us, event | category | flops | bytes accessed | tf_op | source)
XLA Modules:
  0.0 253.2 jit_solution(12796853002330134268)
XLA Ops:
  1.6 2.4 collective-permute-start
  4.9 4.2 %collective-permute-start.1 = (f32[16,256]{1,0:T(8,128)S(1)}, f32[16,256]{1,0:T(8,128)S(1)}, u32[]{:S(2)}, u32[]{:S(2)}) collective-permute-start(f32[16,256]{1,0:T(8,128)S(1)} %bitcast.156), channel_id=1, source_target_pairs={{0,1},{1,2},{2,3},{3,4},{4,5},{5,6},{6,7},{8,9},{9,10},{10,11},{11... | collective-permute-start | bytes 49160 | tf_op jit(solution)/shard_map/ppermute | solution.py:23
  9.2 1.5 fusion.103
  10.7 3.4 %collective-permute-start.3 = (f32[1,64,256]{2,1,0:T(8,128)}, f32[1,64,256]{2,1,0:T(8,128)S(1)}, u32[]{:S(2)}, u32[]{:S(2)}) collective-permute-start(f32[1,64,256]{2,1,0:T(8,128)} %get-tuple-element.62), channel_id=1, source_target_pairs={{0,8},{8,16},{16,24},{1,9},{9,17},{17,25},{2,10},{10,18},{18,26},{... | collective-permute-start | bytes 196616 | tf_op jit(solution)/shard_map/ppermute | solution.py:31
  20.3 1.5 fusion.3
  22.6 5.9 %all-to-all-start = ((f32[3,32,32]{2,0,1:T(4,128)}), f32[3,32,32]{2,0,1:T(4,128)S(1)}, u32[]{:S(2)}, u32[]{:S(2)}) async-start(f32[3,32,32]{2,0,1:T(4,128)} %copy.27), calls=%async_computation | async-start | bytes 131072 | tf_op jit(solution)/shard_map/all_to_all | solution.py:346
  28.6 4.9 %select_maximum_fusion = f32[5,18,66,256]{3,2,1,0:T(8,128)} fusion(f32[1,16,64,256]{3,2,1,0:T(8,128)S(1)} %bitcast.148, f32[1,16,64,256]{3,2,1,0:T(8,128)} %bitcast.149, f32[3,16,64,256]{3,2,1,0:T(8,128)} %param.18), kind=kLoop, calls=%fused_computation.9 | loop fusion | flops 22809600 | bytes 11325440 | tf_op jit(solution)/shard_map/concatenate | solution.py:329
  37.5 10.5 %gather_fusion = f32[1024]{0:T(1024)} fusion(f32[262144]{0:T(1024)S(1)} %bitcast.144, s32[1024]{0:T(1024)S(1)} %broadcast_clamp_fusion), kind=kCustom, calls=%fused_computation | custom fusion | bytes 12288 | tf_op jit(solution)/shard_map/gather | solution.py:360
  48.0 49.6 %fracture_first.1 = (f32[1,1024]{1,0:T(1,128)}, f32[64,128]{1,0:T(8,128)}, f32[8,128]{1,0:T(8,128)}, f32[8,128]{1,0:T(8,128)}) custom-call(f32[1,1024]{1,0:T(1,128)} %bitcast.159, f32[1,1024]{1,0:T(1,128)} %reshape_squeeze.3.refs_1_, s32[1,1024]{1,0:T(1,128)} %convert_element_type.65.refs_2_, f32[8,4,128,128]{3,2,1,0:T(8,128)} %refs_3_.3, s32[8,4]{1,0:T(8,128)} %copy-done.6, ...), custom_call_target="tpu_custom_call" | custom-call | tf_op jit(solution)/shard_map/fracture_first/pallas_call | solution.py:278
  97.7 7.1 %scatter_custom_fusion = f32[262144]{0:T(1024)S(1)} fusion(s32[1024]{0:T(1024)S(1)} %reshape.293, f32[1024]{0:T(1024)} %bitcast.169, f32[]{:T(128)} %constant.101.clone.1), kind=kCustom, calls=%fused_computation.142 | custom fusion | flops 1024 | bytes 1049088 | tf_op jit(solution)/shard_map/scatter-add | solution.py:366
  106.4 2.5 collective-permute-start.5
  110.2 1.5 scatter.6
  111.7 1.7 scatter.9
  113.3 1.5 slice_bitcast_fusion
  114.9 5.8 %broadcast_select_fusion.1 = (f32[16,64,256]{2,1,0:T(8,128)S(1)}, f32[16,64,256]{2,1,0:T(8,128)S(1)}) fusion(pred[16,64]{1,0:T(8,128)(4,1)S(1)} %broadcast_and_fusion, f32[16,64,256]{2,1,0:T(8,128)S(1)} %copy-done, f32[16,64,256]{2,1,0:T(8,128)S(1)} %slice_bitcast_fusion, f32[18,64,256]{2,1,0:T(8,128)} %copy-done.4, ...), kind=kLoop, calls=%fused_computation.139 | loop fusion | flops 7864320 | bytes 12882944 | tf_op jit(solution)/shard_map/jit(_where)/select_n | solution.py:73
  120.8 1.4 collective-permute-start.6
  122.2 3.0 %collective-permute-start.7 = (f32[1,64,256]{2,1,0:T(8,128)S(1)}, f32[1,64,256]{2,1,0:T(8,128)S(1)}, u32[]{:S(2)}, u32[]{:S(2)}) collective-permute-start(f32[1,64,256]{2,1,0:T(8,128)S(1)} %get-tuple-element.59), channel_id=1, source_target_pairs={{0,8},{8,16},{16,24},{1,9},{9,17},{17,25},{2,10},{10,18},{18,26},{... | collective-permute-start | bytes 196616 | tf_op jit(solution)/shard_map/ppermute | solution.py:31
  126.2 4.5 %collective-permute-start.9 = (f32[18,1,256]{2,1,0:T(1,128)S(1)}, f32[18,1,256]{2,1,0:T(1,128)S(1)}, u32[]{:S(2)}, u32[]{:S(2)}) collective-permute-start(f32[18,1,256]{2,1,0:T(1,128)S(1)} %get-tuple-element.52), channel_id=1, source_target_pairs={{0,1},{1,2},{2,3},{3,4},{4,5},{5,6},{6,7},{8,9},{9,10},{10,11},{11... | collective-permute-start | bytes 55304 | tf_op jit(solution)/shard_map/ppermute | solution.py:31
  132.2 4.9 %collective-permute-done.8 = f32[18,1,256]{2,1,0:T(1,128)S(1)} collective-permute-done((f32[18,1,256]{2,1,0:T(1,128)S(1)}, f32[18,1,256]{2,1,0:T(1,128)S(1)}, u32[]{:S(2)}, u32[]{:S(2)}) %collective-permute-start.8) | collective-permute-done | bytes 18464 | tf_op jit(solution)/shard_map/ppermute | solution.py:34
  137.1 3.8 %fusion.77 = f32[16,64,256]{2,1,0:T(8,128)S(1)} fusion(f32[16,64,256]{2,1,0:T(8,128)S(1)} %get-tuple-element.45, f32[16,64,256]{2,1,0:T(8,128)S(1)} %slice_bitcast_fusion, f32[1,64,256]{2,1,0:T(8,128)S(1)} %collective-permute-done.6, f32[1,64,256]{2,1,0:T(8,128)S(1)} %collective-permute-done.7, f32[18,1,256]{2,1,0:T(1,128)S(1)} %collective-permute-done.9, ...), kind=kLoop, calls=%fused_computation.135 | loop fusion | flops 9175040 | bytes 11703296 | tf_op jit(solution)/shard_map/jit(_where)/select_n | solution.py:73
  142.2 3.2 %collective-permute-start.11 = (f32[1,64,256]{2,1,0:T(8,128)S(1)}, f32[1,64,256]{2,1,0:T(8,128)S(1)}, u32[]{:S(2)}, u32[]{:S(2)}) collective-permute-start(f32[1,64,256]{2,1,0:T(8,128)S(1)} %get-tuple-element.57), channel_id=1, source_target_pairs={{0,8},{8,16},{16,24},{1,9},{9,17},{17,25},{2,10},{10,18},{18,26},{... | collective-permute-start | bytes 196616 | tf_op jit(solution)/shard_map/ppermute | solution.py:31
  146.4 4.8 %collective-permute-start.13 = (f32[18,1,256]{2,1,0:T(1,128)S(1)}, f32[18,1,256]{2,1,0:T(1,128)S(1)}, u32[]{:S(2)}, u32[]{:S(2)}) collective-permute-start(f32[18,1,256]{2,1,0:T(1,128)S(1)} %get-tuple-element.50), channel_id=1, source_target_pairs={{0,1},{1,2},{2,3},{3,4},{4,5},{5,6},{6,7},{8,9},{9,10},{10,11},{11... | collective-permute-start | bytes 55304 | tf_op jit(solution)/shard_map/ppermute | solution.py:31
  153.0 10.5 %gather_fusion.1 = f32[1024]{0:T(1024)} fusion(f32[262144]{0:T(1024)S(1)} %bitcast.145, s32[1024]{0:T(1024)S(1)} %broadcast_clamp_fusion), kind=kCustom, calls=%fused_computation.1 | custom fusion | bytes 12288 | tf_op jit(solution)/shard_map/gather | solution.py:360
  163.6 47.5 %fracture_next.1 = (f32[1,1024]{1,0:T(1,128)}, f32[8,128]{1,0:T(8,128)}) custom-call(f32[1,1024]{1,0:T(1,128)} %bitcast.158, f32[1,1024]{1,0:T(1,128)} %reshape_squeeze.3.refs_1_, s32[1,1024]{1,0:T(1,128)} %convert_element_type.65.refs_2_, f32[8,4,128,128]{3,2,1,0:T(8,128)} %refs_3_.3, s32[8,4]{1,0:T(8,128)} %copy-done.6, s32[1,32]{1,0:T(1,128)} %reshape.255.refs_5_, ...), custom_call_target="tpu_custom_call" | custom-call | tf_op jit(solution)/shard_map/fracture_next/pallas_call | solution.py:278
  211.1 7.1 %scatter_custom_fusion.1 = f32[262144]{0:T(1024)S(1)} fusion(s32[1024]{0:T(1024)S(1)} %reshape.293, f32[1024]{0:T(1024)} %bitcast.165, f32[]{:T(128)} %constant.101.clone.1), kind=kCustom, calls=%fused_computation.140 | custom fusion | flops 1024 | bytes 1049088 | tf_op jit(solution)/shard_map/scatter-add | solution.py:366
  219.5 6.2 %broadcast_select_fusion = (f32[16,64,256]{2,1,0:T(8,128)S(1)}, f32[16,64,256]{2,1,0:T(8,128)}) fusion(pred[16,64]{1,0:T(8,128)(4,1)S(1)} %broadcast_and_fusion, f32[16,64,256]{2,1,0:T(8,128)S(1)} %fusion.77, f32[16,64,256]{2,1,0:T(8,128)S(1)} %slice_bitcast_fusion, f32[1,64,256]{2,1,0:T(8,128)S(1)} %collective-permute-done.10, ...), kind=kLoop, calls=%fused_computation.138 | loop fusion | flops 8912896 | bytes 11703296 | tf_op jit(solution)/shard_map/jit(_where)/select_n | solution.py:73
  227.1 3.0 %collective-permute-start.15 = (f32[1,64,256]{2,1,0:T(8,128)S(1)}, f32[1,64,256]{2,1,0:T(8,128)S(1)}, u32[]{:S(2)}, u32[]{:S(2)}) collective-permute-start(f32[1,64,256]{2,1,0:T(8,128)S(1)} %get-tuple-element.55), channel_id=1, source_target_pairs={{0,8},{8,16},{16,24},{1,9},{9,17},{17,25},{2,10},{10,18},{18,26},{... | collective-permute-start | bytes 196616 | tf_op jit(solution)/shard_map/ppermute | solution.py:31
  232.0 2.9 %all-to-all-start.1 = ((f32[32,1,32]{2,1,0:T(1,128)}), f32[32,1,32]{2,1,0:T(1,128)S(1)}, u32[]{:S(2)}, u32[]{:S(2)}) async-start(f32[32,1,32]{2,1,0:T(1,128)} %bitcast.29), calls=%async_computation.1 | async-start | bytes 32768 | tf_op jit(solution)/shard_map/all_to_all | solution.py:370
  235.0 3.7 %collective-permute-start.17 = (f32[18,1,256]{2,1,0:T(1,128)S(1)}, f32[18,1,256]{2,1,0:T(1,128)S(1)}, u32[]{:S(2)}, u32[]{:S(2)}) collective-permute-start(f32[18,1,256]{2,1,0:T(1,128)S(1)} %get-tuple-element.48), channel_id=1, source_target_pairs={{0,1},{1,2},{2,3},{3,4},{4,5},{5,6},{6,7},{8,9},{9,10},{10,11},{11... | collective-permute-start | bytes 55304 | tf_op jit(solution)/shard_map/ppermute | solution.py:31
  240.0 2.1 all-to-all-done.1
  242.8 3.4 %gather_fusion.2 = f32[512]{0:T(512)} fusion(f32[1024]{0:T(1024)S(1)} %reshape.266, s32[1024]{0:T(1024)S(1)} %pad_clamp_fusion), kind=kCustom, calls=%fused_computation.2 | custom fusion | bytes 6144 | tf_op jit(solution)/shard_map/gather | solution.py:373
  246.3 6.4 %fusion.76 = f32[16,64,256]{2,1,0:T(8,128)} fusion(f32[16,64,256]{2,1,0:T(8,128)S(1)} %get-tuple-element.43, f32[16,64,256]{2,1,0:T(8,128)S(1)} %slice_bitcast_fusion, f32[1,64,256]{2,1,0:T(8,128)S(1)} %collective-permute-done.14, f32[1,64,256]{2,1,0:T(8,128)S(1)} %collective-permute-done.15, f32[18,1,256]{2,1,0:T(1,128)S(1)} %collective-permute-done.17, ...), kind=kLoop, calls=%fused_computation.134 | loop fusion | flops 9175040 | bytes 11703296 | tf_op jit(solution)/shard_map/jit(_where)/select_n | solution.py:73
  (100 shorter events, 29.4 us)
Async XLA Ops:
  0.6 27.9 %copy-start.5 = (f32[16,64,256]{2,1,0:T(8,128)S(1)}, f32[16,64,256]{2,1,0:T(8,128)}, u32[]{:S(2)}) copy-start(f32[16,64,256]{2,1,0:T(8,128)} %param.20) | copy-start | bytes 3145732
  1.6 108.6 %collective-permute-start = (f32[64,256]{1,0:T(8,128)S(1)}, f32[64,256]{1,0:T(8,128)S(1)}, u32[]{:S(2)}, u32[]{:S(2)}) collective-permute-start(f32[64,256]{1,0:T(8,128)S(1)} %slice_bitcast_fusion.7), channel_id=1, source_target_pairs={{0,8},{8,16},{16,24},{1,9},{9,17},{17,25},{2,10},{10,18},{18,26},{... | collective-permute-start | bytes 196616 | tf_op jit(solution)/shard_map/ppermute | solution.py:23
  4.9 30.0 %collective-permute-start.1 = (f32[16,256]{1,0:T(8,128)S(1)}, f32[16,256]{1,0:T(8,128)S(1)}, u32[]{:S(2)}, u32[]{:S(2)}) collective-permute-start(f32[16,256]{1,0:T(8,128)S(1)} %bitcast.156), channel_id=1, source_target_pairs={{0,1},{1,2},{2,3},{3,4},{4,5},{5,6},{6,7},{8,9},{9,10},{10,11},{11... | collective-permute-start | bytes 49160 | tf_op jit(solution)/shard_map/ppermute | solution.py:23
  10.7 94.4 %collective-permute-start.3 = (f32[1,64,256]{2,1,0:T(8,128)}, f32[1,64,256]{2,1,0:T(8,128)S(1)}, u32[]{:S(2)}, u32[]{:S(2)}) collective-permute-start(f32[1,64,256]{2,1,0:T(8,128)} %get-tuple-element.62), channel_id=1, source_target_pairs={{0,8},{8,16},{16,24},{1,9},{9,17},{17,25},{2,10},{10,18},{18,26},{... | collective-permute-start | bytes 196616 | tf_op jit(solution)/shard_map/ppermute | solution.py:31
  14.1 91.1 %collective-permute-start.2 = (f32[1,64,256]{2,1,0:T(8,128)S(1)}, f32[1,64,256]{2,1,0:T(8,128)S(1)}, u32[]{:S(2)}, u32[]{:S(2)}) collective-permute-start(f32[1,64,256]{2,1,0:T(8,128)S(1)} %get-tuple-element.61), channel_id=1, source_target_pairs={{8,0},{16,8},{24,16},{9,1},{17,9},{25,17},{10,2},{18,10},{26,18},{... | collective-permute-start | bytes 196616 | tf_op jit(solution)/shard_map/ppermute | solution.py:34
  22.6 13.2 %all-to-all-start = ((f32[3,32,32]{2,0,1:T(4,128)}), f32[3,32,32]{2,0,1:T(4,128)S(1)}, u32[]{:S(2)}, u32[]{:S(2)}) async-start(f32[3,32,32]{2,0,1:T(4,128)} %copy.27), calls=%async_computation | async-start | bytes 131072 | tf_op jit(solution)/shard_map/all_to_all | solution.py:346
  28.6 5.0 %copy-start = (f32[16,64,256]{2,1,0:T(8,128)S(1)}, f32[16,64,256]{2,1,0:T(8,128)}, u32[]{:S(2)}) copy-start(f32[16,64,256]{2,1,0:T(8,128)} %param.17) | copy-start | bytes 3145732
  33.5 0.7 copy-start.9
  34.3 13.8 %copy-start.6 = (s32[8,4]{1,0:T(8,128)}, s32[8,4]{1,0:T(8,128)S(1)}, u32[]{:S(2)}) copy-start(s32[8,4]{1,0:T(8,128)S(1)} %copy.29.refs_4_) | copy-start | bytes 388
  105.0 9.9 %copy-start.1 = (f32[16,64,256]{2,1,0:T(8,128)}, f32[16,64,256]{2,1,0:T(8,128)S(1)}, u32[]{:S(2)}) copy-start(f32[16,64,256]{2,1,0:T(8,128)S(1)} %reshape.260) | copy-start | bytes 3145732
  105.2 1.2 copy-start.4
  106.4 8.5 %collective-permute-start.5 = (f32[18,1,256]{2,1,0:T(1,128)S(1)}, f32[18,1,256]{2,1,0:T(1,128)S(1)}, u32[]{:S(2)}, u32[]{:S(2)}) collective-permute-start(f32[18,1,256]{2,1,0:T(1,128)S(1)} %get-tuple-element.54), channel_id=1, source_target_pairs={{0,1},{1,2},{2,3},{3,4},{4,5},{5,6},{6,7},{8,9},{9,10},{10,11},{11... | collective-permute-start | bytes 55304 | tf_op jit(solution)/shard_map/ppermute | solution.py:31
  108.8 6.1 %collective-permute-start.4 = (f32[18,1,256]{2,1,0:T(1,128)S(1)}, f32[18,1,256]{2,1,0:T(1,128)S(1)}, u32[]{:S(2)}, u32[]{:S(2)}) collective-permute-start(f32[18,1,256]{2,1,0:T(1,128)S(1)} %get-tuple-element.53), channel_id=1, source_target_pairs={{1,0},{2,1},{3,2},{4,3},{5,4},{6,5},{7,6},{9,8},{10,9},{11,10},{12... | collective-permute-start | bytes 55304 | tf_op jit(solution)/shard_map/ppermute | solution.py:34
  113.3 23.7 %slice-start = ((s8[6635520]{0:T(1024)(128)(4,1)}), s8[4194304]{0:T(1024)(128)(4,1)S(1)}, s32[]{:S(2)}) async-start(s8[6635520]{0:T(1024)(128)(4,1)} %bitcast.142), calls=%async_computation.2 | async-start | bytes 8388608
  114.9 22.2 %slice-start.1 = ((s8[6635520]{0:T(1024)(128)(4,1)}), s8[2441216]{0:T(1024)(128)(4,1)S(1)}, s32[]{:S(2)}) async-start(s8[6635520]{0:T(1024)(128)(4,1)} %bitcast.142), calls=%async_computation.3 | async-start | bytes 4882432
  120.7 16.3 %copy-start.2 = (f32[16,64,256]{2,1,0:T(8,128)S(1)}, f32[16,64,256]{2,1,0:T(8,128)}, u32[]{:S(2)}) copy-start(f32[16,64,256]{2,1,0:T(8,128)} %copy-done.1) | copy-start | bytes 3145732
  120.8 4.5 %collective-permute-start.6 = (f32[1,64,256]{2,1,0:T(8,128)S(1)}, f32[1,64,256]{2,1,0:T(8,128)S(1)}, u32[]{:S(2)}, u32[]{:S(2)}) collective-permute-start(f32[1,64,256]{2,1,0:T(8,128)S(1)} %get-tuple-element.60), channel_id=1, source_target_pairs={{8,0},{16,8},{24,16},{9,1},{17,9},{25,17},{10,2},{18,10},{26,18},{... | collective-permute-start | bytes 196616 | tf_op jit(solution)/shard_map/ppermute | solution.py:34
  122.2 3.9 %collective-permute-start.7 = (f32[1,64,256]{2,1,0:T(8,128)S(1)}, f32[1,64,256]{2,1,0:T(8,128)S(1)}, u32[]{:S(2)}, u32[]{:S(2)}) collective-permute-start(f32[1,64,256]{2,1,0:T(8,128)S(1)} %get-tuple-element.59), channel_id=1, source_target_pairs={{0,8},{8,16},{16,24},{1,9},{9,17},{17,25},{2,10},{10,18},{18,26},{... | collective-permute-start | bytes 196616 | tf_op jit(solution)/shard_map/ppermute | solution.py:31
  126.2 6.0 %collective-permute-start.9 = (f32[18,1,256]{2,1,0:T(1,128)S(1)}, f32[18,1,256]{2,1,0:T(1,128)S(1)}, u32[]{:S(2)}, u32[]{:S(2)}) collective-permute-start(f32[18,1,256]{2,1,0:T(1,128)S(1)} %get-tuple-element.52), channel_id=1, source_target_pairs={{0,1},{1,2},{2,3},{3,4},{4,5},{5,6},{6,7},{8,9},{9,10},{10,11},{11... | collective-permute-start | bytes 55304 | tf_op jit(solution)/shard_map/ppermute | solution.py:31
  130.7 6.3 %collective-permute-start.8 = (f32[18,1,256]{2,1,0:T(1,128)S(1)}, f32[18,1,256]{2,1,0:T(1,128)S(1)}, u32[]{:S(2)}, u32[]{:S(2)}) collective-permute-start(f32[18,1,256]{2,1,0:T(1,128)S(1)} %get-tuple-element.51), channel_id=1, source_target_pairs={{1,0},{2,1},{3,2},{4,3},{5,4},{6,5},{7,6},{9,8},{10,9},{11,10},{12... | collective-permute-start | bytes 55304 | tf_op jit(solution)/shard_map/ppermute | solution.py:34
  140.9 4.5 %collective-permute-start.10 = (f32[1,64,256]{2,1,0:T(8,128)S(1)}, f32[1,64,256]{2,1,0:T(8,128)S(1)}, u32[]{:S(2)}, u32[]{:S(2)}) collective-permute-start(f32[1,64,256]{2,1,0:T(8,128)S(1)} %get-tuple-element.58), channel_id=1, source_target_pairs={{8,0},{16,8},{24,16},{9,1},{17,9},{25,17},{10,2},{18,10},{26,18},{... | collective-permute-start | bytes 196616 | tf_op jit(solution)/shard_map/ppermute | solution.py:34
  142.2 4.1 %collective-permute-start.11 = (f32[1,64,256]{2,1,0:T(8,128)S(1)}, f32[1,64,256]{2,1,0:T(8,128)S(1)}, u32[]{:S(2)}, u32[]{:S(2)}) collective-permute-start(f32[1,64,256]{2,1,0:T(8,128)S(1)} %get-tuple-element.57), channel_id=1, source_target_pairs={{0,8},{8,16},{16,24},{1,9},{9,17},{17,25},{2,10},{10,18},{18,26},{... | collective-permute-start | bytes 196616 | tf_op jit(solution)/shard_map/ppermute | solution.py:31
  146.4 73.1 %collective-permute-start.13 = (f32[18,1,256]{2,1,0:T(1,128)S(1)}, f32[18,1,256]{2,1,0:T(1,128)S(1)}, u32[]{:S(2)}, u32[]{:S(2)}) collective-permute-start(f32[18,1,256]{2,1,0:T(1,128)S(1)} %get-tuple-element.50), channel_id=1, source_target_pairs={{0,1},{1,2},{2,3},{3,4},{4,5},{5,6},{6,7},{8,9},{9,10},{10,11},{11... | collective-permute-start | bytes 55304 | tf_op jit(solution)/shard_map/ppermute | solution.py:31
  151.2 68.3 %collective-permute-start.12 = (f32[18,1,256]{2,1,0:T(1,128)S(1)}, f32[18,1,256]{2,1,0:T(1,128)S(1)}, u32[]{:S(2)}, u32[]{:S(2)}) collective-permute-start(f32[18,1,256]{2,1,0:T(1,128)S(1)} %get-tuple-element.49), channel_id=1, source_target_pairs={{1,0},{2,1},{3,2},{4,3},{5,4},{6,5},{7,6},{9,8},{10,9},{11,10},{12... | collective-permute-start | bytes 55304 | tf_op jit(solution)/shard_map/ppermute | solution.py:34
  219.4 11.2 %copy-start.8 = (f32[1,1024]{1,0:T(1,128)S(1)}, f32[1,1024]{1,0:T(1,128)}, u32[]{:S(2)}) copy-start(f32[1,1024]{1,0:T(1,128)} %get-tuple-element.37) | copy-start | bytes 12292
  225.7 20.6 %copy-start.3 = (f32[16,64,256]{2,1,0:T(8,128)S(1)}, f32[16,64,256]{2,1,0:T(8,128)}, u32[]{:S(2)}) copy-start(f32[16,64,256]{2,1,0:T(8,128)} %reshape.264) | copy-start | bytes 3145732
  225.7 9.2 %collective-permute-start.14 = (f32[1,64,256]{2,1,0:T(8,128)S(1)}, f32[1,64,256]{2,1,0:T(8,128)S(1)}, u32[]{:S(2)}, u32[]{:S(2)}) collective-permute-start(f32[1,64,256]{2,1,0:T(8,128)S(1)} %get-tuple-element.56), channel_id=1, source_target_pairs={{8,0},{16,8},{24,16},{9,1},{17,9},{25,17},{10,2},{18,10},{26,18},{... | collective-permute-start | bytes 196616 | tf_op jit(solution)/shard_map/ppermute | solution.py:34
  227.1 7.8 %collective-permute-start.15 = (f32[1,64,256]{2,1,0:T(8,128)S(1)}, f32[1,64,256]{2,1,0:T(8,128)S(1)}, u32[]{:S(2)}, u32[]{:S(2)}) collective-permute-start(f32[1,64,256]{2,1,0:T(8,128)S(1)} %get-tuple-element.55), channel_id=1, source_target_pairs={{0,8},{8,16},{16,24},{1,9},{9,17},{17,25},{2,10},{10,18},{18,26},{... | collective-permute-start | bytes 196616 | tf_op jit(solution)/shard_map/ppermute | solution.py:31
  232.0 10.0 %all-to-all-start.1 = ((f32[32,1,32]{2,1,0:T(1,128)}), f32[32,1,32]{2,1,0:T(1,128)S(1)}, u32[]{:S(2)}, u32[]{:S(2)}) async-start(f32[32,1,32]{2,1,0:T(1,128)} %bitcast.29), calls=%async_computation.1 | async-start | bytes 32768 | tf_op jit(solution)/shard_map/all_to_all | solution.py:370
  235.0 11.3 %collective-permute-start.17 = (f32[18,1,256]{2,1,0:T(1,128)S(1)}, f32[18,1,256]{2,1,0:T(1,128)S(1)}, u32[]{:S(2)}, u32[]{:S(2)}) collective-permute-start(f32[18,1,256]{2,1,0:T(1,128)S(1)} %get-tuple-element.48), channel_id=1, source_target_pairs={{0,1},{1,2},{2,3},{3,4},{4,5},{5,6},{6,7},{8,9},{9,10},{10,11},{11... | collective-permute-start | bytes 55304 | tf_op jit(solution)/shard_map/ppermute | solution.py:31
  238.7 7.6 %collective-permute-start.16 = (f32[18,1,256]{2,1,0:T(1,128)S(1)}, f32[18,1,256]{2,1,0:T(1,128)S(1)}, u32[]{:S(2)}, u32[]{:S(2)}) collective-permute-start(f32[18,1,256]{2,1,0:T(1,128)S(1)} %get-tuple-element.47), channel_id=1, source_target_pairs={{1,0},{2,1},{3,2},{4,3},{5,4},{6,5},{7,6},{9,8},{10,9},{11,10},{12... | collective-permute-start | bytes 55304 | tf_op jit(solution)/shard_map/ppermute | solution.py:34
  246.3 6.4 %copy-start.7 = (f32[8,128]{1,0:T(8,128)S(1)}, f32[8,128]{1,0:T(8,128)}, u32[]{:S(2)}) copy-start(f32[8,128]{1,0:T(8,128)} %get-tuple-element.38) | copy-start | bytes 12292

commit v2 on v0

v2 whole, which is shorter than its diff:
```python
import functools

import jax
import jax.numpy as jnp
from jax import lax
from jax.experimental import pallas as pl
from jax.experimental.pallas import tpu as pltpu
from jax.sharding import PartitionSpec as P

SWEEPS = 2
CG_ITERS = 3
OUTER = 2

EXACT = lax.Precision.HIGHEST
MESH = pl.DeviceIdType.MESH

relax_weight = 0.8


def coupled_kernel(n_frac, n_mat, *refs):
    (press_ref, face_ref, cell_ref, msource_ref, where_ref, kappa_ref, place_ref, tiles_ref, cols_ref, cols_row_ref,
     diag_ref, begin_ref, fsource_ref, out_ref, own_ref, flux_ref, *scratch) = refs
    (gather_ref, outgo_ref, income_ref, mat_ref, back_ref, forth_ref, grid_ref, tx_ref, inv_ref, base_ref, row_hot_ref,
     lane_hot_ref, side_ref, edge_ref, ty_edge_ref, ty_side_ref, gather_send, gather_recv, part_send, part_recv,
     mat_send, mat_recv, halo_send, halo_recv) = scratch
    rows, tiles_row = tiles_ref.shape[0], tiles_ref.shape[1]
    size_b = tiles_ref.shape[3]
    width_x, width_y, depth_z = press_ref.shape
    slots = place_ref.shape[1]
    blocks = rows * n_frac
    sweeps = OUTER * SWEEPS
    phases = CG_ITERS + 1
    me = lax.axis_index("frac")
    me_mat = lax.axis_index("mat")
    mine = pl.ds(pl.multiple_of(me * rows, rows), rows)

    barrier = pltpu.get_barrier_semaphore()
    for k in range(1, n_frac):
        pl.semaphore_signal(barrier, inc=1, device_id={"frac": lax.rem(me + k, n_frac)}, device_id_type=MESH)
    for k in range(1, n_mat):
        pl.semaphore_signal(barrier, inc=1, device_id={"mat": lax.rem(me_mat + k, n_mat)}, device_id_type=MESH)
    pl.semaphore_wait(barrier, n_frac + n_mat - 2)

    sent = []
    pieces = []

    def fill(count):
        for _ in range(min(count, len(pieces))):
            pieces.pop(0)()

    def send(src, dst, send_sem, recv_sem, device):
        copy = pltpu.make_async_remote_copy(
            src_ref=src, dst_ref=dst, send_sem=send_sem, recv_sem=recv_sem, device_id=device, device_id_type=MESH
        )
        copy.start()
        sent.append(copy)
        return copy

    def gather(phase, value):
        gather_ref[phase, mine, :] = value
        here = gather_ref.at[phase, mine]
        return [
            send(here, here, gather_send.at[phase, k - 1], gather_recv.at[phase, k - 1], {"frac": lax.rem(me + k, n_frac)})
            for k in range(1, n_frac)
        ]

    def exchange(phase, low, high, count):
        part = pl.ds(low, high - low)
        copies = []
        for k in range(1, n_frac):
            target = lax.rem(me + k, n_frac)
            copies.append(
                send(
                    outgo_ref.at[phase, target, part],
                    income_ref.at[phase, me, part],
                    part_send.at[phase, k - 1],
                    part_recv.at[phase, k - 1],
                    {"frac": target},
                )
            )
        income_ref[phase, me, part, :] = outgo_ref[phase, me, part, :]
        fill(count)
        for copy in copies:
            copy.wait_recv()
        total = income_ref[phase, 0, part, :]
        for k in range(1, n_frac):
            total = total + income_ref[phase, k, part, :]
        return total

    def products(phase, with_back):
        def row(r, carry):
            across = gather_ref[phase, pl.ds(me * rows + r, 1), :]
            down = jnp.broadcast_to(across, (size_b, size_b)).T
            total = jnp.zeros((size_b, size_b), jnp.float32)
            for t in range(tiles_row):
                tile = tiles_ref[r, t]
                total = total + tile * gather_ref[phase, pl.ds(cols_ref[r, t], 1), :]
                if with_back:
                    back_ref[pl.ds(r * tiles_row + t, 1), :] = jnp.sum(tile * down, axis=0, keepdims=True)
            forth_ref[pl.ds(r, 1), :] = jnp.sum(total.T, axis=0, keepdims=True)
            return carry

        lax.fori_loop(0, rows, row, 0)
        forward = forth_ref[...]
        if not with_back:
            return forward, None
        named = lax.broadcasted_iota(jnp.int32, (blocks, rows * tiles_row), 0) == cols_row_ref[...]
        spread = jnp.dot(named.astype(jnp.float32), back_ref[...], precision=EXACT, preferred_element_type=jnp.float32)
        return forward, spread

    def total_of(values):
        return jnp.sum(values, axis=(0, 1), keepdims=True)

    def thirds(values):
        high = values.astype(jnp.bfloat16)
        rest = values - high.astype(jnp.float32)
        middle = rest.astype(jnp.bfloat16)
        return high, middle, (rest - middle.astype(jnp.float32)).astype(jnp.bfloat16)

    lanes = lax.broadcasted_iota(jnp.int32, (width_y, depth_z), 1)
    lines = lax.broadcasted_iota(jnp.int32, (width_y, depth_z), 0)
    next_mat, prev_mat = lax.rem(me_mat + 1, n_mat), lax.rem(me_mat + n_mat - 1, n_mat)
    next_frac, prev_frac = lax.rem(me + 1, n_frac), lax.rem(me + n_frac - 1, n_frac)
    halos = {}

    def send_halo(sweep, last, first):
        sems = [(halo_send.at[sweep, d], halo_recv.at[sweep, d]) for d in range(4)]
        halos[sweep] = [
            send(last, grid_ref.at[sweep, 0], *sems[0], {"mat": next_mat}),
            send(first, grid_ref.at[sweep, width_x + 1], *sems[1], {"mat": prev_mat}),
            send(edge_ref.at[sweep, 0], side_ref.at[sweep, 0], *sems[2], {"frac": next_frac}),
            send(edge_ref.at[sweep, 1], side_ref.at[sweep, 1], *sems[3], {"frac": prev_frac}),
        ]

    def wait_halo(sweep):
        for copy in halos[sweep]:
            copy.wait_recv()
        grid_ref[sweep, 0] = jnp.where(me_mat == 0, 0.0, grid_ref[sweep, 0])
        grid_ref[sweep, width_x + 1] = jnp.where(me_mat == n_mat - 1, 0.0, grid_ref[sweep, width_x + 1])
        side_ref[sweep, 0] = jnp.where(me == 0, 0.0, side_ref[sweep, 0])
        side_ref[sweep, 1] = jnp.where(me == n_frac - 1, 0.0, side_ref[sweep, 1])

    def tz_inner(x):
        return jnp.where(lanes == depth_z - 1, 0.0, face_ref[2, x])

    def set_inverse():
        for copy in coef_copies:
            copy.wait_recv()
        tx_ref[0] = jnp.where(me_mat == 0, 0.0, tx_ref[0])
        ty_side_ref[...] = jnp.where(me == 0, 0.0, ty_side_ref[...])

        def plane(x, carry):
            tx_here, ty_here = face_ref[0, x], face_ref[1, x]
            tx_ref[x + 1] = tx_here
            ty_low = jnp.where(lines == 0, ty_side_ref[pl.ds(x, 1), :], pltpu.roll(ty_here, 1, 0))
            tz_low = pltpu.roll(tz_inner(x), 1, 1)
            inv_ref[x] = relax_weight / (cell_ref[x] + tx_here + tx_ref[x] + ty_here + ty_low + face_ref[2, x] + tz_low)
            return carry

        lax.fori_loop(0, width_x, plane, 0)

    def sweep_part(sweep, low, high):
        def plane(x, carry):
            here = grid_ref[sweep, x + 1]
            ty_here, tz_here = face_ref[1, x], tz_inner(x)
            up = jnp.where(lines == width_y - 1, side_ref[sweep, 1, pl.ds(x, 1), :], pltpu.roll(here, width_y - 1, 0))
            down = jnp.where(
                lines == 0,
                ty_side_ref[pl.ds(x, 1), :] * side_ref[sweep, 0, pl.ds(x, 1), :],
                pltpu.roll(ty_here * here, 1, 0),
            )
            total = base_ref[x] + tx_ref[x + 1] * grid_ref[sweep, x + 2] + tx_ref[x] * grid_ref[sweep, x]
            total = total + ty_here * up + down
            total = total + tz_here * pltpu.roll(here, depth_z - 1, 1) + pltpu.roll(tz_here * here, 1, 1)
            value = (1.0 - relax_weight) * here + inv_ref[x] * total
            if sweep + 1 < sweeps:
                grid_ref[sweep + 1, x + 1] = value
                edge_ref[sweep + 1, 0, pl.ds(x, 1), :] = value[width_y - 1 :]
                edge_ref[sweep + 1, 1, pl.ds(x, 1), :] = value[:1]
            else:
                out_ref[x] = value
            return carry

        lax.fori_loop(low, high, plane, 0)

    quarter = width_x // 4

    def set_sources(low, parts):
        hot = row_hot_ref[low * width_y : (low + quarter) * width_y, :]
        total = sum(
            lax.dot_general(hot, part, (((1,), (1,)), ((), ())), preferred_element_type=jnp.float32) for part in parts
        )
        base_ref[low : low + quarter] = msource_ref[low : low + quarter] + total.reshape(quarter, width_y, depth_z)

    def add_sweep(sweep):
        pieces.append(lambda: wait_halo(sweep))
        for q in range(4):
            pieces.append(functools.partial(sweep_part, sweep, q * quarter, (q + 1) * quarter))
        if sweep + 1 < sweeps:
            pieces.append(
                lambda: send_halo(sweep + 1, grid_ref.at[sweep + 1, width_x], grid_ref.at[sweep + 1, 1])
            )

    def traces(sweep):
        found = []
        cut = slots // 4
        parts = thirds(grid_ref[sweep, 1 : width_x + 1].reshape(width_x * width_y, depth_z))
        for q in range(4):
            hot = row_hot_ref[:, q * cut : (q + 1) * cut]
            picked = sum(
                lax.dot_general(part, hot, (((0,), (0,)), ((), ())), preferred_element_type=jnp.float32)
                for part in parts
            )
            mask = lane_hot_ref[:, q * cut : (q + 1) * cut].astype(jnp.float32)
            found.append(jnp.sum(picked * mask, axis=0, keepdims=True))
        return jnp.concatenate(found, axis=1)

    begin = begin_ref[...]
    first_copies = gather(0, begin)
    grid_ref[0, 1 : width_x + 1] = press_ref[...]
    edge_ref[0, 0] = press_ref[:, width_y - 1, :]
    edge_ref[0, 1] = press_ref[:, 0, :]
    ty_edge_ref[...] = face_ref[1, :, width_y - 1, :]
    coef_copies = [
        send(face_ref.at[0, width_x - 1], tx_ref.at[0], halo_send.at[sweeps, 0], halo_recv.at[sweeps, 0], {"mat": next_mat}),
        send(ty_edge_ref, ty_side_ref, halo_send.at[sweeps, 2], halo_recv.at[sweeps, 2], {"frac": next_frac}),
    ]
    send_halo(0, press_ref.at[width_x - 1], press_ref.at[0])
    place = place_ref[...]
    block_of = place // size_b
    lane_of = place - block_of * size_b
    by_block = (lax.broadcasted_iota(jnp.int32, (blocks, slots), 0) == block_of).astype(jnp.float32)
    by_lane = (lax.broadcasted_iota(jnp.int32, (size_b, slots), 0) == lane_of).astype(jnp.float32)
    cell = where_ref[...]
    cell_row = cell // depth_z
    cell_lane = cell - cell_row * depth_z

    row_hot_ref[...] = (lax.broadcasted_iota(jnp.int32, row_hot_ref.shape, 0) == cell_row).astype(jnp.float32).astype(jnp.bfloat16)
    lane_hot_ref[...] = (lax.broadcasted_iota(jnp.int32, lane_hot_ref.shape, 0) == cell_lane).astype(jnp.float32).astype(jnp.bfloat16)

    diag = diag_ref[...]
    for outer_no in range(OUTER):
        first = outer_no == 0
        stage = outer_no * phases
        trace = traces(outer_no * SWEEPS)
        if first:
            for copy in first_copies:
                copy.wait_recv()
            fracture = gather_ref[0]
        picked = lax.dot_general(fracture, by_block, (((0,), (0,)), ((), ())), precision=EXACT, preferred_element_type=jnp.float32)
        flux = kappa_ref[...] * (trace - jnp.sum(picked * by_lane, axis=0, keepdims=True))
        landed = lax.dot_general(by_block * flux, by_lane, (((1,), (1,)), ((), ())), precision=EXACT, preferred_element_type=jnp.float32)
        if first:
            forward, spread = products(0, True)
        for k in range(n_frac):
            if first:
                outgo_ref[stage, k, 0:rows, :] = spread[k * rows : (k + 1) * rows]
            outgo_ref[stage, k, rows : 2 * rows, :] = landed[k * rows : (k + 1) * rows]
        parts = [lane_hot_ref[...] * part for part in thirds(flux)]
        if first:
            pieces.append(set_inverse)
        for q in range(4):
            pieces.append(functools.partial(set_sources, q * quarter, parts))
        for s in range(SWEEPS):
            add_sweep(outer_no * SWEEPS + s)
        both = exchange(stage, 0 if first else rows, 2 * rows, 2)
        if first:
            image = diag * begin + 0.5 * (forward + both[0:rows])
        mat_ref[outer_no, me_mat] = both[rows:] if first else both
        slot = mat_ref.at[outer_no, me_mat]
        copies = [
            send(slot, slot, mat_send.at[outer_no, k - 1], mat_recv.at[outer_no, k - 1], {"mat": lax.rem(me_mat + k, n_mat)})
            for k in range(1, n_mat)
        ]
        fill(2)
        for copy in copies:
            copy.wait_recv()
        load = mat_ref[outer_no, 0]
        for k in range(1, n_mat):
            load = load + mat_ref[outer_no, k]
        if first:
            residual = fsource_ref[...] + load - image
        else:
            residual = residual + (load - loaded)
        loaded = load

        for step in range(CG_ITERS):
            phase = stage + step + 1
            needed = first or step + 1 < CG_ITERS
            copies = gather(phase, residual)
            fill(2)
            for copy in copies:
                copy.wait_recv()
            whole = gather_ref[phase]
            forward, spread = products(phase, needed)
            inner = residual * (diag * residual + forward)
            for k in range(n_frac):
                if needed:
                    outgo_ref[phase, k, 0:rows, :] = spread[k * rows : (k + 1) * rows]
                outgo_ref[phase, k, rows : 2 * rows, :] = inner
            both = exchange(phase, 0 if needed else rows, 2 * rows, 3)
            if needed:
                image = diag * residual + 0.5 * (forward + both[0:rows])
                product = total_of(both[rows : 2 * rows])
            else:
                product = total_of(both)
            norm_next = total_of(whole * whole)
            if step == 0:
                alpha = norm_next / product
                direction = whole
                along = image
            else:
                ratio = norm_next / norm_now
                alpha = norm_next / (product - ratio * norm_next / alpha)
                direction = whole + ratio * direction
                if needed:
                    along = image + ratio * along
            norm_now = norm_next
            fracture = fracture + alpha * direction
            if needed:
                residual = residual - alpha * along
        fill(len(pieces))
    flux_ref[...] = flux
    gather_ref[phases] = fracture
    own_ref[...] = gather_ref[phases, mine, :]
    for copy in sent:
        copy.wait_send()


def coupled(pressure, face, cell_coef, matrix_source, cells, kappa, place, tiles, tile_cols, diag, begin, fsource):
    n_frac, n_mat = lax.axis_size("frac"), lax.axis_size("mat")
    rows, tiles_row, size_b = tiles.shape[0], tiles.shape[1], tiles.shape[3]
    blocks = rows * n_frac
    x, y, z = pressure.shape
    slots = cells.shape[1]
    f32 = jnp.float32
    vmem = pl.BlockSpec(memory_space=pltpu.VMEM)
    smem = pl.BlockSpec(memory_space=pltpu.SMEM)
    phases = OUTER * (CG_ITERS + 1)
    sweeps = OUTER * SWEEPS
    dma = pltpu.SemaphoreType.DMA
    return pl.pallas_call(
        functools.partial(coupled_kernel, n_frac, n_mat),
        out_shape=(
            jax.ShapeDtypeStruct((x, y, z), f32),
            jax.ShapeDtypeStruct((rows, size_b), f32),
            jax.ShapeDtypeStruct((1, slots), f32),
        ),
        in_specs=[vmem] * 8 + [smem] + [vmem] * 4,
        out_specs=(vmem,) * 3,
        scratch_shapes=[
            pltpu.VMEM((phases, blocks, size_b), f32),
            pltpu.VMEM((phases, n_frac, 2 * rows, size_b), f32),
            pltpu.VMEM((phases, n_frac, 2 * rows, size_b), f32),
            pltpu.VMEM((OUTER, n_mat, rows, size_b), f32),
            pltpu.VMEM((rows * tiles_row, size_b), f32),
            pltpu.VMEM((rows, size_b), f32),
            pltpu.VMEM((sweeps, x + 2, y, z), f32),
            pltpu.VMEM((x + 1, y, z), f32),
            pltpu.VMEM((x, y, z), f32),
            pltpu.VMEM((x, y, z), f32),
            pltpu.VMEM((x * y, slots), jnp.bfloat16),
            pltpu.VMEM((z, slots), jnp.bfloat16),
            pltpu.VMEM((sweeps, 2, x, z), f32),
            pltpu.VMEM((sweeps, 2, x, z), f32),
            pltpu.VMEM((x, z), f32),
            pltpu.VMEM((x, z), f32),
            dma((phases, n_frac - 1)),
            dma((phases, n_frac - 1)),
            dma((phases, n_frac - 1)),
            dma((phases, n_frac - 1)),
            dma((OUTER, n_mat - 1)),
            dma((OUTER, n_mat - 1)),
            dma((sweeps + 1, 4)),
            dma((sweeps + 1, 4)),
        ],
        compiler_params=pltpu.CompilerParams(
            collective_id=0, has_side_effects=True, vmem_limit_bytes=60 * 1024 * 1024
        ),
        name="coupled",
    )(pressure, face, cell_coef, matrix_source, cells, kappa, place, tiles, tile_cols, tile_cols.reshape(1, -1), diag, begin, fsource)


def body(
    pressure_start,
    face_trans,
    cell_coef,
    matrix_source,
    mortar_owner,
    mortar_cell,
    mortar_frac,
    mortar_kappa,
    tiles,
    tile_cols,
    frac_diag,
    frac_source,
    fracture_start,
):
    mat_count = lax.axis_size("mat")
    frac_count = lax.axis_size("frac")
    devices = mat_count * frac_count
    size_b = tiles.shape[2]
    owner = mortar_owner[:, 0]
    mortar_count = owner.shape[0]
    capacity = max(2, 2 * mortar_count // devices)
    hits = (owner[:, None] == jnp.arange(devices, dtype=jnp.int32)[None, :]).astype(jnp.int32)
    ranks = jnp.cumsum(hits, axis=0)
    slot = jnp.sum(ranks * hits, axis=1) - 1
    place = owner * capacity + slot
    slots = devices * capacity
    at_slot = (place[:, None] == jnp.arange(slots, dtype=jnp.int32)[None, :]).astype(jnp.float32)
    payload = jnp.stack([mortar_cell.astype(jnp.float32), mortar_frac.astype(jnp.float32), mortar_kappa])
    outgoing = jnp.dot(payload, at_slot, precision=EXACT).reshape(3, devices, capacity)
    incoming = lax.all_to_all(outgoing, ("mat", "frac"), split_axis=1, concat_axis=1, tiled=True)
    cell_slots = jnp.round(incoming[0]).astype(jnp.int32).reshape(1, -1)
    frac_slots = jnp.round(incoming[1]).astype(jnp.int32).reshape(1, -1)
    kappa_slots = incoming[2].reshape(1, -1)
    blocked = (-1, size_b)
    pressure, fracture, flux = coupled(
        pressure_start,
        face_trans,
        cell_coef,
        matrix_source,
        cell_slots,
        kappa_slots,
        frac_slots,
        tiles,
        tile_cols,
        frac_diag.reshape(blocked),
        fracture_start.reshape(blocked),
        frac_source.reshape(blocked),
    )
    returned = lax.all_to_all(
        flux.reshape(devices, capacity), ("mat", "frac"), split_axis=0, concat_axis=0, tiled=True
    )
    return (pressure, fracture.reshape(-1), returned.reshape(-1)[place])


def solution(mesh):
    in_specs = (
        P("mat", "frac", None),
        P(None, "mat", "frac", None),
        P("mat", "frac", None),
        P("mat", "frac", None),
        P(("mat", "frac"), None),
        P(("mat", "frac")),
        P(("mat", "frac")),
        P(("mat", "frac")),
        P("frac", None, None, None),
        P("frac", None),
        P("frac"),
        P("frac"),
        P("frac"),
    )
    out_specs = (P("mat", "frac", None), P("frac"), P(("mat", "frac")))
    return jax.shard_map(body, mesh=mesh, in_specs=in_specs, out_specs=out_specs, check_vma=False)
```

time: 988 us -> 133 us (0.13)
  blocking collectives: 725 us -> 0 us
  Pallas kernels: 0 us -> 90.2 us
  other arithmetic: 79.7 us -> 6.86 us
  starting transfers between devices: 61.8 us -> 9.87 us
  local copies, waits for them, and re-layouts: 60.8 us -> 10.7 us
  matrix products: 23.6 us -> 1.5 us
  between operations: 22.3 us -> 0.71 us
    unnamed x8 -> x0, blocking collectives: 291 us -> none
    all_gather x8 -> x0, blocking collectives: 246 us -> none  [the longest x6 184 us: fracture_apply(): whole = lax.all_gather(vector, 'frac', axis=0, tiled=True)]
    psum x8 -> x0, blocking collectives: 188 us -> none  [the longest x6 107 us: two_products(): lax.psum((jnp.sum(residual * residual), jnp.sum(residual * image)), 'frac')]
    pallas_call x0 -> x1, Pallas kernels: none -> 90.2 us  [coupled(): pl.pallas_call(functools.partial(coupled_kernel, n_frac, n_mat), out_shap...]
    ppermute x18 -> x0, starting transfers between devices: 40.7 us -> none  [the longest x8 23.7 us: with_halo(): lax.ppermute(lax.slice_in_dim(block, block.shape[dim] - width, None, axis...]
    select_n x9 -> x1, other arithmetic: 35.9 us -> 0.69 us  [body(): return (pressure, fracture.reshape(-1), returned.reshape(-1)[place])]
    scatter-add x12 -> x0, other arithmetic: 29.3 us -> none  [the longest x2 16.1 us: body(): jax.ops.segment_sum(arrived.reshape(-1), asked_safe.reshape(-1), num_segm...]
    gather x14 -> x1, local copies, waits for them, and re-layouts: 27.7 us -> 3.41 us  [body(): return (pressure, fracture.reshape(-1), returned.reshape(-1)[place])]
  transfers between devices with their start and end apart: 23 -> 2, of which waited for: 2 -> 2; matrix products, arithmetic and copies ran while one was open for 12% -> 1% of each run, Pallas kernels for 0% -> 0%
where the time goes in v2:
time: 133 us
  Pallas kernels  90.2 us (68%)
  waiting for transfers between devices  13 us (10%)
  local copies, waits for them, and re-layouts  10.7 us (8%)
  starting transfers between devices  9.87 us (7%)
  other arithmetic  6.86 us (5%)
  matrix products  1.5 us (1%)
    pallas_call x1, Pallas kernels, coupled(): pl.pallas_call(functools.partial(coupled_kernel, n_frac, n_mat), out_shap...  90.2 us
    all_to_all x1, starting transfers between devices, body(): lax.all_to_all(outgoing, ('mat', 'frac'), split_axis=1, concat_axis=1, ti...  7.33 us
    all_to_all x1, waiting for transfers between devices, body(): lax.all_to_all(flux.reshape(devices, capacity), ('mat', 'frac'), split_ax...  7.06 us
    all_to_all x1, waiting for transfers between devices, body(): lax.all_to_all(outgoing, ('mat', 'frac'), split_axis=1, concat_axis=1, ti...  5.92 us
    gather x1, local copies, waits for them, and re-layouts, body(): return (pressure, fracture.reshape(-1), returned.reshape(-1)[place])  3.41 us
  transfers between devices with their start and end apart: 2, of which 2 were waited for; matrix products, arithmetic and copies ran while one was open for 1% of the time, Pallas kernels for 0%

profile of v2, /device:TPU:0, one launch (start us, length us, event | category | flops | bytes accessed | tf_op | source)
XLA Modules:
  0.0 132.8 jit_solution(8462458740805564474)
XLA Ops:
  0.6 0.7 fusion.4
  1.3 1.2 reduce-window.6
  2.5 0.2 slice_reduce_fusion
  2.7 0.8 fusion.3
  3.5 0.7 compare_select_fusion
  4.2 0.7 convert_element_type.38
  4.9 0.7 convert_element_type.39
  5.6 1.5 %fusion = f32[3,1024]{1,0:T(4,128)S(1)} fusion(s32[512]{0:T(512)S(1)} %bitcast.38, f32[1,512]{1,0:T(1,128)} %bitcast.39, f32[1,512]{1,0:T(1,128)S(1)} %bitcast.37, f32[1,512]{1,0:T(1,128)S(1)} %bitcast.36), kind=kOutput, calls=%fused_computation.2 | convolution fusion | flops 19401728 | bytes 20480 | tf_op jit(solution)/shard_map/dot_general | solution.py:413
  7.1 0.1 reshape.91
  7.2 0.7 copy.22
  7.9 7.3 %all-to-all-start = ((f32[3,32,32]{2,0,1:T(4,128)}), f32[3,32,32]{2,0,1:T(4,128)S(1)}, u32[]{:S(2)}, u32[]{:S(2)}) async-start(f32[3,32,32]{2,0,1:T(4,128)} %copy.22), calls=%async_computation | async-start | bytes 131072 | tf_op jit(solution)/shard_map/all_to_all | solution.py:414
  15.2 0.8 copy.24.refs_8_
  16.0 0.6 reshape.92.refs_9_
  16.5 5.9 %all-to-all-done = f32[3,32,32]{2,0,1:T(4,128)S(1)} async-done(((f32[3,32,32]{2,0,1:T(4,128)}), f32[3,32,32]{2,0,1:T(4,128)S(1)}, u32[]{:S(2)}, u32[]{:S(2)}) %all-to-all-start) | async-done | bytes 12320 | tf_op jit(solution)/shard_map/all_to_all | solution.py:414
  22.5 0.1 fusion.6
  22.6 0.7 convert_element_type.42.refs_4_
  23.2 0.7 convert_element_type.44.refs_6_
  23.9 0.1 slice_reduce_fusion.1
  24.0 0.7 reshape_squeeze.3.refs_5_
  24.6 0.0 copy-done.1
  24.6 90.2 %coupled.1 = (f32[16,64,256]{2,1,0:T(8,128)}, f32[8,128]{1,0:T(8,128)}, f32[1,1024]{1,0:T(1,128)}) custom-call(f32[16,64,256]{2,1,0:T(8,128)} %refs_0_.1, f32[3,16,64,256]{3,2,1,0:T(8,128)} %refs_1_.1, f32[16,64,256]{2,1,0:T(8,128)} %refs_2_.1, f32[16,64,256]{2,1,0:T(8,128)} %refs_3_.1, s32[1,1024]{1,0:T(1,128)} %convert_element_type.42.refs_4_, ...), custom_call_target="tpu_custom_call" | custom-call | tf_op jit(solution)/shard_map/coupled/pallas_call | solution.py:342
  114.9 0.0 copy-start
  114.9 0.5 broadcast.57
  115.4 1.3 %reduce.20 = f32[1024]{0:T(1024)S(1)} reduce(f32[1,1024]{1,0:T(1,128)} %get-tuple-element.8, f32[]{:T(128)} %broadcast.57), dimensions={0}, to_apply=%get-tuple-element.8.reduce_sub_computation.3 | reduce | bytes 8196 | tf_op jit(solution)/shard_map/coupled/pallas_call | solution.py:342
  116.7 0.7 all_to_all.10
  117.4 2.5 %all-to-all-start.1 = ((f32[32,1,32]{2,1,0:T(1,128)}), f32[32,1,32]{2,1,0:T(1,128)S(1)}, u32[]{:S(2)}, u32[]{:S(2)}) async-start(f32[32,1,32]{2,1,0:T(1,128)} %bitcast.12), calls=%async_computation.1 | async-start | bytes 32768 | tf_op jit(solution)/shard_map/all_to_all | solution.py:433
  120.0 7.1 %all-to-all-done.1 = f32[32,1,32]{2,1,0:T(1,128)S(1)} async-done(((f32[32,1,32]{2,1,0:T(1,128)}), f32[32,1,32]{2,1,0:T(1,128)S(1)}, u32[]{:S(2)}, u32[]{:S(2)}) %all-to-all-start.1) | async-done | bytes 4128 | tf_op jit(solution)/shard_map/all_to_all | solution.py:433
  127.0 0.7 reduce.21
  127.7 0.1 reshape.97
  127.8 3.4 %gather_fusion = f32[512]{0:T(512)} fusion(f32[1024]{0:T(1024)S(1)} %reshape.97, s32[1024]{0:T(1024)S(1)} %pad_clamp_fusion), kind=kCustom, calls=%fused_computation | custom fusion | bytes 6144 | tf_op jit(solution)/shard_map/gather | solution.py:436
  131.2 1.0 copy.30
  132.2 0.6 copy.31
  (8 shorter events, 0.1 us)
Async XLA Ops:
  7.9 14.6 %all-to-all-start = ((f32[3,32,32]{2,0,1:T(4,128)}), f32[3,32,32]{2,0,1:T(4,128)S(1)}, u32[]{:S(2)}, u32[]{:S(2)}) async-start(f32[3,32,32]{2,0,1:T(4,128)} %copy.22), calls=%async_computation | async-start | bytes 131072 | tf_op jit(solution)/shard_map/all_to_all | solution.py:414
  16.0 8.7 %copy-start.1 = (s32[8,4]{1,0:T(8,128)}, s32[8,4]{1,0:T(8,128)S(1)}, u32[]{:S(2)}) copy-start(s32[8,4]{1,0:T(8,128)S(1)} %copy.24.refs_8_) | copy-start | bytes 388
  114.9 16.3 %copy-start = (f32[16,64,256]{2,1,0:T(8,128)S(1)}, f32[16,64,256]{2,1,0:T(8,128)}, u32[]{:S(2)}) copy-start(f32[16,64,256]{2,1,0:T(8,128)} %get-tuple-element.16) | copy-start | bytes 3145732
  117.4 9.6 %all-to-all-start.1 = ((f32[32,1,32]{2,1,0:T(1,128)}), f32[32,1,32]{2,1,0:T(1,128)S(1)}, u32[]{:S(2)}, u32[]{:S(2)}) async-start(f32[32,1,32]{2,1,0:T(1,128)} %bitcast.12), calls=%async_computation.1 | async-start | bytes 32768 | tf_op jit(solution)/shard_map/all_to_all | solution.py:433
  127.8 4.4 %copy-start.2 = (f32[8,128]{1,0:T(8,128)S(1)}, f32[8,128]{1,0:T(8,128)}, u32[]{:S(2)}) copy-start(f32[8,128]{1,0:T(8,128)} %get-tuple-element.7) | copy-start | bytes 12292
